TPU v7x, 128 devices: a whole 4x4x4 slice. The times are simulated.
128 devices in a mesh: gx: 8 (over x, core), yz: 16 (over z, y).
Axes of the slice: x: 4, y: 4, z: 4, core: 2. Of those that a mesh axis runs over, the one named last changes fastest.
Arguments:
- fine_blocks: bfloat16 [1024, 1536, 512], P(('gx', 'yz')), may hold values from -6 to 6
- fine_to_coarse: int32 [1024], replicated, may hold values from 0 to 511, as said below
- widths: int32 [1024], P(('gx', 'yz')), may hold values from 256 to 512
- pivots: int32 [512, 1024], P(('gx', 'yz')), may hold values from 0 to 1023, as said below
- neighbours: int32 [512, 4], P(('gx', 'yz')), may hold values from 0 to 3
Outputs:
- interp: float32 [512, 384, 640], P(('gx', 'yz'))
- schur_blocks: float32 [512, 384, 384], P(('gx', 'yz'))
Inputs may be any that keep to these rules, and one draw needn't show every extreme that they name: `fine_to_coarse`: cluster c is owned by the device of index c // 4 along gx+yz, which has the same gx index as both its fine blocks; each cluster has exactly two fine blocks, on different devices, and the 8 blocks of one device belong to clusters of 8 different devices. `pivots`: each row is a permutation of 0 to 1023 whose first 384 entries are live columns (below the width of the first block, or 512 plus a column below the width of the second).
All inputs are finite; a program needn't handle non-finite values.
Results may differ from a plain program's by a relative error of at most 0.0003.
Values may be sent and summed in bfloat16 or wider, within the bound.
A program may use at most 192 MiB of HBM per device.

v0:
```python
import jax
import jax.numpy as jnp
from jax import lax
from jax.sharding import PartitionSpec as P

K = 384


def in_blocks(x, dim, length):
    dims = x.shape
    tiles = x.reshape(*dims[:dim], length, dims[dim] // length, *dims[dim + 1 :])
    return jnp.moveaxis(tiles, dim, 0)


def cut_rows(length, count):
    hop = length // count
    if hop >= 8:
        hop -= hop % 8
    return [hop * k for k in range(1, count)]


def laid_out(tiles, dim):
    tiles = jnp.moveaxis(tiles, 0, dim)
    dims = tiles.shape
    return tiles.reshape(*dims[:dim], dims[dim] * dims[dim + 1], *dims[dim + 2 :])


def exchange_in_pieces(x, axis, pieces, split_dim, concat_dim):
    tiles = in_blocks(x, split_dim, lax.axis_size(axis))
    cut = max(range(1, max(2, tiles.ndim - 1)), key=lambda d: tiles.shape[d])
    finished = []
    for slab in jnp.split(tiles, cut_rows(tiles.shape[cut], pieces), axis=cut):
        if slab.size:
            finished.append(lax.all_to_all(slab, axis, split_axis=0, concat_axis=0, tiled=True))
    return laid_out(jnp.concatenate(finished, axis=cut), concat_dim)


def with_halo(x, sides, width):
    edges = {}
    for axis, dim in sides:
        size, length = (lax.axis_size(axis), x.shape[dim])
        up = [(i, (i + 1) % size) for i in range(size - 1)]
        last = lax.slice_in_dim(x, length - width, length, axis=dim)
        leading = lax.slice_in_dim(x, 0, width, axis=dim)
        edges[dim] = (
            lax.ppermute(last, axis, up),
            lax.ppermute(leading, axis, [(b, a) for a, b in up]),
        )
    done = []
    for _, dim in sides:
        low, high = edges[dim]
        around = [(width, width) if d in done else (0, 0) for d in range(x.ndim)]
        x = jnp.concatenate([jnp.pad(low, around), x, jnp.pad(high, around)], axis=dim)
        done.append(dim)
    return x


def interpolate(gram_rows, kept_cols):
    factor = jnp.linalg.cholesky(gram_rows[:, :, :kept_cols])
    half_solved = jax.scipy.linalg.solve_triangular(factor, gram_rows[:, :, kept_cols:], lower=True)
    return jax.scipy.linalg.solve_triangular(factor, half_solved, lower=True, trans=1)


def pick_sides(nearby, neighbours):
    side_terms = jnp.stack([nearby[0, 1], nearby[2, 1], nearby[1, 0], nearby[1, 2]])
    cluster_count = side_terms.shape[1]
    flattened = side_terms.reshape((4 * cluster_count,) + side_terms.shape[2:])
    flat_index = jnp.arange(4, dtype=jnp.int32)[None, :] * cluster_count + neighbours
    chosen = jnp.take(flattened, flat_index.reshape(-1), axis=0)
    return chosen.reshape((cluster_count, 4) + side_terms.shape[2:])


def body(fine_blocks, fine_to_coarse, widths, pivots, neighbours):
    gx_count = lax.axis_size("gx")
    yz_count = lax.axis_size("yz")
    gx_pos = lax.axis_index("gx")
    yz_pos = lax.axis_index("yz")
    blocks_dev = fine_blocks.shape[0]
    col_count = fine_blocks.shape[2]
    clusters = blocks_dev // 2
    kept_cols = K
    device = gx_pos * yz_count + yz_pos
    cluster_table = fine_to_coarse.reshape(gx_count, yz_count, blocks_dev)
    grouped = lax.dynamic_index_in_dim(cluster_table, gx_pos, 0, keepdims=False)
    own_targets = lax.dynamic_index_in_dim(grouped, yz_pos, 0, keepdims=False)
    target = own_targets // clusters - gx_pos * yz_count
    column = jnp.arange(col_count, dtype=jnp.int32)
    live_cols = (column[None, :] < widths[:, None]).astype(jnp.bfloat16)
    masked = fine_blocks * live_cols[:, None, :]
    peer_ids = jnp.arange(yz_count, dtype=jnp.int32)
    matches = target[None, :] == peer_ids[:, None]
    source_slot = jnp.sum(
        jnp.where(matches, jnp.arange(blocks_dev, dtype=jnp.int32)[None, :], 0), axis=1
    )
    filled = jnp.any(matches, axis=1).astype(jnp.bfloat16)
    outgoing = jnp.take(masked, source_slot, axis=0) * filled[:, None, None]
    arrived = exchange_in_pieces(outgoing, "yz", 2, 0, 0)
    owned_here = grouped // clusters == device
    local_index = jnp.sum(jnp.where(owned_here, grouped % clusters, 0), axis=1)
    arrived_any = jnp.any(owned_here, axis=1)
    member = arrived_any[None, :] & (
        local_index[None, :] == jnp.arange(clusters, dtype=jnp.int32)[:, None]
    )
    first_src = jnp.min(jnp.where(member, peer_ids[None, :], yz_count), axis=1)
    second = jnp.max(jnp.where(member, peer_ids[None, :], -1), axis=1)
    merged = jnp.concatenate(
        [jnp.take(arrived, first_src, axis=0), jnp.take(arrived, second, axis=0)], axis=2
    )
    pivoted = jnp.take_along_axis(merged, pivots[:, None, :], axis=2)
    gram_rows = jnp.einsum(
        "cpk,cpw->ckw", pivoted[:, :, :kept_cols], pivoted, preferred_element_type=jnp.float32
    )
    interp = interpolate(gram_rows, kept_cols)
    updates = jnp.einsum("ckr,cjr->ckj", interp, interp, precision=lax.Precision.HIGHEST)
    nearby = with_halo(updates[None, None], (("gx", 0), ("yz", 1)), 1)
    chosen = pick_sides(nearby, neighbours)
    schur_blocks = updates + jnp.sum(chosen, axis=1)
    return (interp, schur_blocks)


def solution(mesh):
    return jax.shard_map(
        body,
        mesh=mesh,
        in_specs=(
            P(("gx", "yz"), None, None),
            P(),
            P(("gx", "yz")),
            P(("gx", "yz"), None),
            P(("gx", "yz"), None),
        ),
        out_specs=(P(("gx", "yz"), None, None), P(("gx", "yz"), None, None)),
        check_vma=False,
    )
```

profile of v0, /device:TPU:10, one launch (start us, length us, event | category | flops | bytes accessed | tf_op | source)
XLA Modules:
  0.0 1063.9 jit_solution(2705907405660198310)
XLA Ops:
  2.4 10.6 broadcast_multiply_fusion
  13.0 14.6 %gather_fusion = bf16[16,1536,512]{2,1,0:T(8,128)(2,1)} fusion(bf16[8,1536,512]{2,1,0:T(8,128)(2,1)} %broadcast_multiply_fusion, s32[1024]{0:T(1024)S(1)} %pad_clamp_fusion.3), kind=kCustom, calls=%fused_computation.2 | custom fusion | bytes 50331712 | tf_op jit(solution)/shard_map/jit(_take)/gather | solution.py:96
  27.6 12.6 %fusion = bf16[16,1,1536,512]{3,2,1,0:T(8,128)(2,1)S(1)} fusion(bf16[16,1536,512]{2,1,0:T(8,128)(2,1)} %gather_fusion, pred[16]{0:T(512)(128)(4,1)S(1)} %compare_and_fusion.4, bf16[16]{0:T(256)(128)(2,1)S(1)} %convert_element_type.18), kind=kLoop, calls=%fused_computation.9 | loop fusion | flops 25165824 | bytes 50331696 | tf_op jit(solution)/shard_map/mul | solution.py:96
  40.2 8.7 fusion.58
  48.9 147.9 %all_to_all.10 = bf16[16,1,768,512]{3,2,1,0:T(8,128)(2,1)} all-to-all(bf16[16,1,768,512]{3,2,1,0:T(8,128)(2,1)} %get-tuple-element.30), channel_id=1, replica_groups=mesh['gx'=8,'yz'=16] {'yz'}, dimensions={0} | all-to-all | bytes 25165824 | tf_op jit(solution)/shard_map/all_to_all | solution.py:34
  196.8 6.3 all-to-all-start.1
  204.7 179.0 %all-to-all-done.1 = bf16[16,1,768,512]{3,2,1,0:T(8,128)(2,1)} async-done(((bf16[16,1,768,512]{3,2,1,0:T(8,128)(2,1)}), bf16[16,1,768,512]{3,2,1,0:T(8,128)(2,1)}, u32[]{:S(2)}, u32[]{:S(2)}) %all-to-all-start.1) | async-done | bytes 12582944 | tf_op jit(solution)/shard_map/all_to_all | solution.py:34
  383.7 25.6 %maximum_bitcast_fusion = bf16[16,1536,512]{2,1,0:T(8,128)(2,1)} fusion(bf16[16,1,768,512]{3,2,0,1:T(8,128)(2,1)} %bitcast.6, bf16[16,1,768,512]{3,2,0,1:T(8,128)(2,1)} %bitcast.126), kind=kLoop, calls=%fused_computation.7 | loop fusion | flops 50331648 | bytes 50331648 | tf_op jit(solution)/shard_map/reshape | solution.py:25
  409.3 11.8 %gather_fusion.3 = bf16[4,1536,512]{2,1,0:T(8,128)(2,1)} fusion(bf16[16,1536,512]{2,1,0:T(8,128)(2,1)} %maximum_bitcast_fusion, s32[1024]{0:T(1024)S(1)} %pad_clamp_fusion.2), kind=kCustom, calls=%fused_computation.clone | custom fusion | bytes 12582928 | tf_op jit(solution)/shard_map/jit(_take)/gather | solution.py:107
  421.1 11.8 %gather_fusion.4 = bf16[4,1536,512]{2,1,0:T(8,128)(2,1)} fusion(bf16[16,1536,512]{2,1,0:T(8,128)(2,1)} %maximum_bitcast_fusion, s32[1024]{0:T(1024)S(1)} %pad_clamp_fusion.1), kind=kCustom, calls=%fused_computation.1.clone | custom fusion | bytes 12582928 | tf_op jit(solution)/shard_map/jit(_take)/gather | solution.py:107
  433.0 3.6 broadcast_select_fusion.3
  440.8 8.5 pad_maximum_fusion
  449.3 16.7 %copy.46 = bf16[4,1536,1024]{1,2,0:T(8,128)(2,1)} copy(bf16[4,1536,1024]{2,1,0:T(8,128)(2,1)} %pad_maximum_fusion) | data formatting | bytes 25165824 | tf_op jit(solution)/shard_map/concatenate | solution.py:106
  466.0 91.6 %gather_fusion.2 = bf16[4096,1536]{1,0:T(8,128)(2,1)} fusion(bf16[4,1536,1024]{1,2,0:T(8,128)(2,1)} %copy.46, s32[4096]{0:T(1024)S(1)} %bitcast.123), kind=kCustom, calls=%fused_computation.4 | custom fusion | bytes 25198592 | tf_op jit(solution)/shard_map/jit(take_along_axis)/gather | solution.py:109
  557.6 10.9 %fusion.2 = bf16[4,1536,1024]{1,2,0:T(8,128)(2,1)} fusion(bf16[4,1024,1536]{2,1,0:T(8,128)(2,1)} %bitcast.124, pred[4,1024]{1,0:T(4,128)(4,1)S(1)} %compare_and_fusion), kind=kLoop, calls=%fused_computation.13 | loop fusion | flops 6291456 | bytes 25169920 | tf_op jit(solution)/shard_map/jit(take_along_axis)/select_n | solution.py:109
  568.5 9.1 fusion.1
  587.3 47.4 %custom-call.29 = f32[4,128,128]{2,1,0:T(8,128)S(1)} custom-call(f32[4,128,128]{2,1,0:T(8,128)S(1)} %cholesky.198), custom_call_target="Cholesky" | custom-call | tf_op jit(solution)/shard_map/jit(cholesky)/cholesky | solution.py:59
  634.9 39.3 %custom-call.30 = f32[4,1,128,128]{2,3,1,0:T(8,128)S(1)} custom-call(f32[4,1,128,128]{3,2,1,0:T(8,128)S(1)} %select_bitcast_fusion.1), custom_call_target="InvertDiagBlocksLowerTriangular" | custom-call | tf_op jit(solution)/shard_map/jit(cholesky)/cholesky | solution.py:59
  678.3 47.7 %custom-call.31 = f32[4,128,128]{2,1,0:T(8,128)S(1)} custom-call(f32[4,128,128]{2,1,0:T(8,128)} %cholesky.202), custom_call_target="Cholesky" | custom-call | tf_op jit(solution)/shard_map/jit(cholesky)/cholesky | solution.py:59
  727.5 40.9 %custom-call.32 = f32[4,1,128,128]{2,3,1,0:T(8,128)} custom-call(f32[4,1,128,128]{3,2,1,0:T(8,128)} %get-tuple-element.33), custom_call_target="InvertDiagBlocksLowerTriangular" | custom-call | tf_op jit(solution)/shard_map/jit(cholesky)/cholesky | solution.py:59
  771.3 46.9 %custom-call.33 = f32[4,128,128]{2,1,0:T(8,128)S(1)} custom-call(f32[4,128,128]{2,1,0:T(8,128)S(1)} %convolution_subtract_fusion.3), custom_call_target="Cholesky" | custom-call | tf_op jit(solution)/shard_map/jit(cholesky)/cholesky | solution.py:59
  821.1 11.1 %while.1 = (s32[]{:T(128)}, f32[4,384,384]{2,1,0:T(8,128)}, s32[3,2]{0,1:T(2,128)S(1)}, f32[3,4,128,128]{3,2,0,1:T(8,128)}, s32[]{:T(128)}) while((s32[]{:T(128)}, f32[4,384,384]{2,1,0:T(8,128)}, s32[3,2]{0,1:T(2,128)S(1)}, f32[3,4,128,128]{3,2,0,1:T(8,128)}, s32[]{:T(128)}) %tuple.35), condition=%wide.while_cond, body=%wide.while_body.sunk | while | flops 2 | bytes 525921 | solution.py:61
  832.3 119.1 %custom-call.34 = f32[4,3,128,128]{2,3,1,0:T(8,128)S(1)} custom-call(f32[4,3,128,128]{3,2,1,0:T(8,128)} %bitcast.132), custom_call_target="InvertDiagBlocksLowerTriangular" | custom-call | tf_op jit(solution)/shard_map/jit(_solve_triangular)/vmap()/triangular_solve | solution.py:61
  969.7 7.3 fusion.59
  979.0 3.6 collective-permute-start.1
  984.7 5.3 collective-permute-start.3
  990.1 17.2 %collective-permute-done = f32[1,1,4,384,384]{4,3,2,1,0:T(8,128)} collective-permute-done((f32[1,1,4,384,384]{4,3,2,1,0:T(8,128)S(1)}, f32[1,1,4,384,384]{4,3,2,1,0:T(8,128)}, u32[]{:S(2)}, u32[]{:S(2)}) %collective-permute-start) | collective-permute-done | bytes 2359328 | tf_op jit(solution)/shard_map/ppermute | solution.py:46
  1009.0 28.5 %collective-permute-done.2 = f32[1,1,4,384,384]{4,3,2,1,0:T(8,128)} collective-permute-done((f32[1,1,4,384,384]{4,3,2,1,0:T(8,128)S(1)}, f32[1,1,4,384,384]{4,3,2,1,0:T(8,128)}, u32[]{:S(2)}, u32[]{:S(2)}) %collective-permute-start.2) | collective-permute-done | bytes 2359328 | tf_op jit(solution)/shard_map/ppermute | solution.py:46
  1037.5 4.5 collective-permute-done.3
  1041.9 6.5 pad_maximum_fusion.1
  1048.4 8.5 gather_fusion.1
  1056.9 4.8 select_reduce_fusion
  (93 shorter events, 65.7 us)
Async XLA Ops:
  196.8 6.4 copy-start.6
  196.8 187.0 %all-to-all-start.1 = ((bf16[16,1,768,512]{3,2,1,0:T(8,128)(2,1)}), bf16[16,1,768,512]{3,2,1,0:T(8,128)(2,1)}, u32[]{:S(2)}, u32[]{:S(2)}) async-start(bf16[16,1,768,512]{3,2,1,0:T(8,128)(2,1)} %get-tuple-element.31), calls=%async_computation.1 | async-start | bytes 25165824 | tf_op jit(solution)/shard_map/all_to_all | solution.py:34
  204.0 430.8 %copy-start.5 = (pred[128,128]{1,0:T(8,128)(4,1)}, pred[128,128]{1,0:T(8,128)(4,1)S(1)}, u32[]{:S(2)}) copy-start(pred[128,128]{1,0:T(8,128)(4,1)S(1)} %iota_compare_fusion.1) | copy-start | bytes 49156
  433.0 4.6 copy-start.1
  577.6 2.7 copy-start.2
  585.9 1.4 copy-start.4
  819.4 1.8 copy-start.8
  832.3 121.7 %copy-start.3 = (f32[4,384,384]{2,1,0:T(8,128)S(1)}, f32[4,384,384]{2,1,0:T(8,128)}, u32[]{:S(2)}) copy-start(f32[4,384,384]{2,1,0:T(8,128)} %get-tuple-element.87) | copy-start | bytes 7077892
  969.7 7.4 copy-start
  969.7 20.3 %copy-start.7 = (s32[4,4]{1,0:T(4,128)S(1)}, s32[4,4]{1,0:T(4,128)}, u32[]{:S(2)}) copy-start(s32[4,4]{1,0:T(4,128)} %param.11) | copy-start | bytes 196
  977.1 30.3 %collective-permute-start = (f32[1,1,4,384,384]{4,3,2,1,0:T(8,128)S(1)}, f32[1,1,4,384,384]{4,3,2,1,0:T(8,128)}, u32[]{:S(2)}, u32[]{:S(2)}) collective-permute-start(f32[1,1,4,384,384]{4,3,2,1,0:T(8,128)S(1)} %bitcast.128), channel_id=1, source_target_pairs={{0,16},{16,32},{32,48},{48,64},{64,80},{80,96},{96,112},{1,17},{17... | collective-permute-start | bytes 7077896 | tf_op jit(solution)/shard_map/ppermute | solution.py:46
  979.0 30.0 %collective-permute-start.1 = (f32[1,1,4,384,384]{4,3,2,1,0:T(8,128)S(1)}, f32[1,1,4,384,384]{4,3,2,1,0:T(8,128)}, u32[]{:S(2)}, u32[]{:S(2)}) collective-permute-start(f32[1,1,4,384,384]{4,3,2,1,0:T(8,128)S(1)} %bitcast.129), channel_id=1, source_target_pairs={{16,0},{32,16},{48,32},{64,48},{80,64},{96,80},{112,96},{17,1},{33... | collective-permute-start | bytes 7077896 | tf_op jit(solution)/shard_map/ppermute | solution.py:47
  982.6 54.8 %collective-permute-start.2 = (f32[1,1,4,384,384]{4,3,2,1,0:T(8,128)S(1)}, f32[1,1,4,384,384]{4,3,2,1,0:T(8,128)}, u32[]{:S(2)}, u32[]{:S(2)}) collective-permute-start(f32[1,1,4,384,384]{4,3,2,1,0:T(8,128)S(1)} %bitcast.130), channel_id=1, source_target_pairs={{0,1},{1,2},{2,3},{3,4},{4,5},{5,6},{6,7},{7,8},{8,9},{9,10},{10,1... | collective-permute-start | bytes 7077896 | tf_op jit(solution)/shard_map/ppermute | solution.py:46
  984.7 57.2 %collective-permute-start.3 = (f32[1,1,4,384,384]{4,3,2,1,0:T(8,128)S(1)}, f32[1,1,4,384,384]{4,3,2,1,0:T(8,128)}, u32[]{:S(2)}, u32[]{:S(2)}) collective-permute-start(f32[1,1,4,384,384]{4,3,2,1,0:T(8,128)S(1)} %bitcast.131), channel_id=1, source_target_pairs={{1,0},{2,1},{3,2},{4,3},{5,4},{6,5},{7,6},{8,7},{9,8},{10,9},{11,1... | collective-permute-start | bytes 7077896 | tf_op jit(solution)/shard_map/ppermute | solution.py:47
where the time goes:
time: 1080 us; the launch traced here: 1060 us
  other arithmetic  439 us (41%)
  waiting for transfers between devices  231 us (21%)
  local copies, waits for them, and re-layouts  185 us (17%)
  blocking collectives  148 us (14%)
  matrix products  40.7 us (4%)
  starting transfers between devices  19.2 us (2%)
    another operation x14, other arithmetic, interpolate(): factor = jnp.linalg.cholesky(gram_rows[:, :, :kept_cols])  225 us
    all_to_all x1, waiting for transfers between devices, exchange_in_pieces(): lax.all_to_all(slab, axis, split_axis=0, concat_axis=0, tiled=True)  179 us
    all_to_all x1, blocking collectives, exchange_in_pieces(): lax.all_to_all(slab, axis, split_axis=0, concat_axis=0, tiled=True)  148 us
    another operation x5, other arithmetic, interpolate(): jax.scipy.linalg.solve_triangular(factor, half_solved, lower=True, trans=1)  122 us
    gather x1, local copies, waits for them, and re-layouts, body(): pivoted = jnp.take_along_axis(merged, pivots[:, None, :], axis=2)  91.6 us
    ppermute x2, waiting for transfers between devices, with_halo(): lax.ppermute(last, axis, up)  45.7 us
    reshape x1, other arithmetic, laid_out(): tiles.reshape(*dims[:dim], dims[dim] * dims[dim + 1], *dims[dim + 2:])  25.6 us
  transfers between devices with their start and end apart: 5, of which 5 were waited for; matrix products, arithmetic and copies ran while one was open for 0% of the time, Pallas kernels for 0%

commit v1 on v0

v1 whole, which is shorter than its diff:
```python
import functools

import jax
import jax.numpy as jnp
from jax import lax
from jax.experimental import pallas as pl
from jax.experimental.pallas import tpu as pltpu
from jax.sharding import PartitionSpec as P

K = 384
HIGH = lax.Precision.HIGHEST


def iota(shape, dim):
    return lax.broadcasted_iota(jnp.int32, shape, dim)


def place_kernel(target_ref, widths_ref, x_ref, o_ref):
    b = pl.program_id(0)
    x = x_ref[0]
    live = iota(x.shape, 1) < widths_ref[b]
    o_ref[0] = jnp.where(live, x, jnp.zeros_like(x))


def place_blocks(fine_blocks, target, widths, peers):
    count, rows, cols = fine_blocks.shape
    return pl.pallas_call(
        place_kernel,
        out_shape=jax.ShapeDtypeStruct((peers, rows, cols), fine_blocks.dtype),
        grid_spec=pltpu.PrefetchScalarGridSpec(
            num_scalar_prefetch=2,
            grid=(count,),
            in_specs=[pl.BlockSpec((1, rows, cols), lambda b, t, w: (b, 0, 0))],
            out_specs=pl.BlockSpec((1, rows, cols), lambda b, t, w: (t[b], 0, 0)),
        ),
        name="place_blocks",
    )(target, widths, fine_blocks)


def gram_kernel(first_ref, second_ref, a_ref, b_ref, piv_ref, o_ref, hot_ref):
    r = pl.program_id(1)
    half = a_ref.shape[2]

    @pl.when(r == 0)
    def _():
        hot_ref[...] = jnp.where(iota(hot_ref.shape, 0) == piv_ref[0], 1.0, 0.0).astype(hot_ref.dtype)

    pivoted = jnp.dot(a_ref[0], hot_ref[:half, :], preferred_element_type=jnp.float32)
    pivoted += jnp.dot(b_ref[0], hot_ref[half:, :], preferred_element_type=jnp.float32)
    pivoted = pivoted.astype(jnp.bfloat16)
    part = lax.dot_general(
        pivoted[:, :K], pivoted, (((0,), (0,)), ((), ())), preferred_element_type=jnp.float32
    )

    @pl.when(r == 0)
    def _():
        o_ref[0] = part

    @pl.when(r > 0)
    def _():
        o_ref[0] += part


def gram_of(arrived, first, second, pivots):
    peers, rows, half = arrived.shape
    clusters, width = pivots.shape
    step = 512
    return pl.pallas_call(
        gram_kernel,
        out_shape=jax.ShapeDtypeStruct((clusters, K, width), jnp.float32),
        grid_spec=pltpu.PrefetchScalarGridSpec(
            num_scalar_prefetch=2,
            grid=(clusters, rows // step),
            in_specs=[
                pl.BlockSpec((1, step, half), lambda c, r, f, s: (f[c], r, 0)),
                pl.BlockSpec((1, step, half), lambda c, r, f, s: (s[c], r, 0)),
                pl.BlockSpec((1, 1, width), lambda c, r, f, s: (c, 0, 0)),
            ],
            out_specs=pl.BlockSpec((1, K, width), lambda c, r, f, s: (c, 0, 0)),
            scratch_shapes=[pltpu.VMEM((width, width), jnp.bfloat16)],
        ),
        name="pivot_gram",
    )(first, second, arrived, arrived, pivots[:, None, :])


def packed_inverse(s):
    lane, row = iota(s.shape, 1), iota(s.shape, 0)
    inner = lane % 32
    base = lane - inner
    for k in range(32):
        col = jnp.take_along_axis(s, base + k, axis=1)
        here = inner == k
        scale = 1.0 / jnp.broadcast_to(col[k : k + 1], s.shape)
        scaled = jnp.where(here, scale, jnp.broadcast_to(s[k : k + 1], s.shape) * scale)
        s = jnp.where(row == k, scaled, jnp.where(here, 0.0, s) - col * scaled)
    return s


def invert_diagonal(d_ref):
    lane, row = iota((128, 128), 1), iota((128, 128), 0)
    lane32 = iota((32, 128), 1)
    for q in range(4):
        lo, hi = 32 * q, 32 * q + 32
        packed = jnp.zeros((32, 128), jnp.float32)
        for c in range(4):
            rows = d_ref[c, lo:hi, :]
            moved = pltpu.roll(rows, (32 * (c - q)) % 128, 1) if c != q else rows
            packed = jnp.where(lane32 // 32 == c, moved, packed)
        packed = packed_inverse(packed)
        in_cols = (lane >= lo) & (lane < hi)
        in_rows = (row >= lo) & (row < hi)
        in_lanes = (lane32 >= lo) & (lane32 < hi)
        for c in range(4):
            moved = pltpu.roll(packed, (32 * (q - c)) % 128, 1) if c != q else packed
            inverse = jnp.where(in_lanes, moved, 0.0)
            d = d_ref[c]
            scaled = jnp.dot(inverse, d, precision=HIGH, preferred_element_type=jnp.float32)
            scaled = jnp.where(in_lanes, inverse, scaled)
            parts = ([jnp.zeros((lo, 128), jnp.float32)] if lo else []) + [scaled]
            parts += [jnp.zeros((128 - hi, 128), jnp.float32)] if hi < 128 else []
            full = jnp.concatenate(parts, axis=0) if len(parts) > 1 else scaled
            lhs = jnp.where(in_cols & ~in_rows, -d, 0.0)
            kept = jnp.where(in_cols | in_rows, 0.0, d) + full
            d_ref[c] = kept + jnp.dot(lhs, full, precision=HIGH, preferred_element_type=jnp.float32)


def solve_kernel(g_ref, interp_ref, update_ref, w_ref, d_ref):
    clusters, width = g_ref.shape[0], g_ref.shape[2]
    w_ref[...] = g_ref[...]

    def eliminate(s, carry):
        at = pl.ds(pl.multiple_of(s * 128, 128), 128)
        for c in range(clusters):
            d_ref[c] = w_ref[c, at, at]
        invert_diagonal(d_ref)

        def one(c, carry):
            scaled = jnp.dot(d_ref[c], w_ref[c, at, :], precision=HIGH, preferred_element_type=jnp.float32)
            w_ref[c, at, :] = scaled
            for far in range(1, K // 128):
                other = lax.rem(s + far, K // 128)
                rows = pl.ds(pl.multiple_of(other * 128, 128), 128)
                w_ref[c, rows, :] = w_ref[c, rows, :] - jnp.dot(
                    w_ref[c, rows, at], scaled, precision=HIGH, preferred_element_type=jnp.float32
                )
            return carry

        return lax.fori_loop(0, clusters, one, carry)

    lax.fori_loop(0, K // 128, eliminate, 0)

    def finish(c, carry):
        x = w_ref[c, :, K:]
        interp_ref[c] = x
        update_ref[c] = lax.dot_general(
            x, x, (((1,), (1,)), ((), ())), precision=HIGH, preferred_element_type=jnp.float32
        )
        return carry

    lax.fori_loop(0, clusters, finish, 0)


def solve(gram):
    clusters, kept, width = gram.shape
    return pl.pallas_call(
        solve_kernel,
        out_shape=(
            jax.ShapeDtypeStruct((clusters, kept, width - kept), jnp.float32),
            jax.ShapeDtypeStruct((clusters, kept, kept), jnp.float32),
        ),
        in_specs=[pl.BlockSpec(memory_space=pltpu.VMEM)],
        out_specs=(pl.BlockSpec(memory_space=pltpu.VMEM), pl.BlockSpec(memory_space=pltpu.VMEM)),
        scratch_shapes=[
            pltpu.VMEM((clusters, kept, width), jnp.float32),
            pltpu.VMEM((clusters, 128, 128), jnp.float32),
        ],
        compiler_params=pltpu.CompilerParams(vmem_limit_bytes=56 * 1024 * 1024),
        name="solve_update",
    )(gram)


def schur_kernel(n_ref, own_ref, a_ref, b_ref, c_ref, d_ref, o_ref):
    o_ref[...] = own_ref[...] + ((a_ref[...] + b_ref[...]) + (c_ref[...] + d_ref[...]))


def gather_schur(update, sides, neighbours):
    clusters, kept, _ = update.shape

    def pick(side):
        return pl.BlockSpec((1, kept, kept), lambda c, n: (n[4 * c + side], 0, 0))

    own = pl.BlockSpec((1, kept, kept), lambda c, n: (c, 0, 0))
    return pl.pallas_call(
        schur_kernel,
        out_shape=jax.ShapeDtypeStruct(update.shape, jnp.float32),
        grid_spec=pltpu.PrefetchScalarGridSpec(
            num_scalar_prefetch=1,
            grid=(clusters,),
            in_specs=[own] + [pick(side) for side in range(4)],
            out_specs=own,
        ),
        name="gather_schur",
    )(neighbours.reshape(-1), update, *sides)


def from_sides(x):
    sides = []
    for axis in ("gx", "yz"):
        size = lax.axis_size(axis)
        up = [(i, i + 1) for i in range(size - 1)]
        sides += [lax.ppermute(x, axis, up), lax.ppermute(x, axis, [(b, a) for a, b in up])]
    return sides


def body(fine_blocks, fine_to_coarse, widths, pivots, neighbours):
    gx_count, yz_count = lax.axis_size("gx"), lax.axis_size("yz")
    gx_pos, yz_pos = lax.axis_index("gx"), lax.axis_index("yz")
    blocks_dev = fine_blocks.shape[0]
    clusters = blocks_dev // 2
    grouped = lax.dynamic_index_in_dim(
        fine_to_coarse.reshape(gx_count, yz_count, blocks_dev), gx_pos, 0, keepdims=False
    )
    owner, local = grouped // clusters - gx_pos * yz_count, grouped % clusters
    target = lax.dynamic_index_in_dim(owner, yz_pos, 0, keepdims=False)
    mine = (owner == yz_pos)[None] & (local[None] == jnp.arange(clusters, dtype=jnp.int32)[:, None, None])
    peer = jnp.arange(yz_count, dtype=jnp.int32)[None, :, None]
    first = jnp.min(jnp.where(mine, peer, yz_count - 1), axis=(1, 2))
    second = jnp.max(jnp.where(mine, peer, 0), axis=(1, 2))
    placed = place_blocks(fine_blocks, target, widths, yz_count)
    arrived = lax.all_to_all(placed, "yz", split_axis=0, concat_axis=0, tiled=True)
    interp, update = solve(gram_of(arrived, first, second, pivots))
    return interp, gather_schur(update, from_sides(update), neighbours)


def solution(mesh):
    split = ("gx", "yz")
    return jax.shard_map(
        body,
        mesh=mesh,
        in_specs=(P(split, None, None), P(), P(split), P(split, None), P(split, None)),
        out_specs=(P(split, None, None), P(split, None, None)),
        check_vma=False,
    )
```

time: 1080 us -> 577 us (0.53); the launches traced: 1060 us -> 573 us
  other arithmetic: 439 us -> 0.87 us
  waiting for transfers between devices: 231 us -> 416 us
  local copies, waits for them, and re-layouts: 185 us -> 2.77 us
  blocking collectives: 148 us -> 0 us
  Pallas kernels: 0 us -> 126 us
  matrix products: 40.7 us -> 0 us
    another operation x20 -> x0, other arithmetic: 354 us -> none  [the longest x14 225 us: interpolate(): factor = jnp.linalg.cholesky(gram_rows[:, :, :kept_cols])]
    all_to_all x1, waiting for transfers between devices: 179 us -> 367 us  [body(): lax.all_to_all(placed, 'yz', split_axis=0, concat_axis=0, tiled=True)]
    all_to_all x1 -> x0, blocking collectives: 148 us -> none  [exchange_in_pieces(): lax.all_to_all(slab, axis, split_axis=0, concat_axis=0, tiled=True)]
    gather x5 -> x0, local copies, waits for them, and re-layouts: 138 us -> none  [the longest x1 91.6 us: body(): pivoted = jnp.take_along_axis(merged, pivots[:, None, :], axis=2)]
    pallas_call x0 -> x4, Pallas kernels: none -> 126 us  [the longest x1 81 us: solve(): pl.pallas_call(solve_kernel, out_shape=(jax.ShapeDtypeStruct((clusters, k...]
    reshape x1 -> x0, other arithmetic: 25.6 us -> none  [laid_out(): tiles.reshape(*dims[:dim], dims[dim] * dims[dim + 1], *dims[dim + 2:])]
    another operation x14 -> x0, matrix products: 24.3 us -> none  [the longest x5 10.9 us: interpolate(): jax.scipy.linalg.solve_triangular(factor, gram_rows[:, :, kept_cols:], lo...]
    mul x3 -> x0, other arithmetic: 23.2 us -> none  [the longest x1 12.6 us: body(): outgoing = jnp.take(masked, source_slot, axis=0) * filled[:, None, None]]
where the time goes in v1:
time: 577 us; the launch traced here: 573 us
  waiting for transfers between devices  416 us (72%)
  Pallas kernels  126 us (22%)
  starting transfers between devices  26.9 us (5%)
    all_to_all x1, waiting for transfers between devices, body(): lax.all_to_all(placed, 'yz', split_axis=0, concat_axis=0, tiled=True)  367 us
    pallas_call x1, Pallas kernels, solve(): pl.pallas_call(solve_kernel, out_shape=(jax.ShapeDtypeStruct((clusters, k...  81 us
    ppermute x2, waiting for transfers between devices, from_sides(): lax.ppermute(x, axis, up)  45 us
    pallas_call x1, Pallas kernels, gram_of(): pl.pallas_call(gram_kernel, out_shape=jax.ShapeDtypeStruct((clusters, K,...  26.7 us
    ppermute x2, starting transfers between devices, from_sides(): lax.ppermute(x, axis, [(b, a) for a, b in up])  14.2 us
    pallas_call x1, Pallas kernels, place_blocks(): pl.pallas_call(place_kernel, out_shape=jax.ShapeDtypeStruct((peers, rows,...  12.1 us
  transfers between devices with their start and end apart: 5, of which 5 were waited for; matrix products, arithmetic and copies ran while one was open for 0% of the time, Pallas kernels for 0%

profile of v1, /device:TPU:10, one launch (start us, length us, event | category | flops | bytes accessed | tf_op | source)
XLA Modules:
  0.0 573.4 jit_solution(5101398228765605420)
XLA Ops:
  0.6 0.8 reshape.10
  1.4 0.1 copy.18
  1.5 0.7 dynamic-slice_reduce_fusion.target_ref
  2.2 12.1 %place_blocks.1 = bf16[16,1536,512]{2,1,0:T(8,128)(2,1)} custom-call(s32[8]{0:T(128)} %dynamic-slice_reduce_fusion.target_ref, s32[8]{0:T(128)} %widths_ref.1, bf16[8,1536,512]{2,1,0:T(8,128)(2,1)} %x_ref.1), custom_call_target="tpu_custom_call" | custom-call | tf_op jit(solution)/shard_map/place_blocks/pallas_call | solution.py:27
  14.3 0.0 copy-start.1
  14.3 8.5 %all-to-all-start = ((bf16[16,1536,512]{2,1,0:T(8,128)(2,1)}), bf16[16,1536,512]{2,1,0:T(8,128)(2,1)}, u32[]{:S(2)}, u32[]{:S(2)}) async-start(bf16[16,1536,512]{2,1,0:T(8,128)(2,1)} %place_blocks.1), calls=%async_computation | async-start | bytes 50331648 | tf_op jit(solution)/shard_map/all_to_all | solution.py:230
  22.8 0.0 copy-done.1
  22.8 0.6 broadcast_in_dim.31.piv_ref
  23.5 0.8 select_reduce_fusion
  24.3 366.6 %all-to-all-done.a_ref.b_ref = bf16[16,1536,512]{2,1,0:T(8,128)(2,1)} async-done(((bf16[16,1536,512]{2,1,0:T(8,128)(2,1)}), bf16[16,1536,512]{2,1,0:T(8,128)(2,1)}, u32[]{:S(2)}, u32[]{:S(2)}) %all-to-all-start) | async-done | bytes 25165856 | tf_op jit(solution)/shard_map/all_to_all | solution.py:230
  390.9 26.7 %pivot_gram.1.g_ref = f32[4,384,1024]{2,1,0:T(8,128)} custom-call(s32[4]{0:T(128)} %get-tuple-element.7.first_ref, s32[4]{0:T(128)} %get-tuple-element.6.second_ref, bf16[16,1536,512]{2,1,0:T(8,128)(2,1)} %all-to-all-done.a_ref.b_ref, bf16[16,1536,512]{2,1,0:T(8,128)(2,1)} %all-to-all-done.a_ref.b_ref, s32[4,1,1024]{2,1,0:T(1,128)} %broadcast_in_dim.31.piv_ref), custom_call_target="tpu_custom_call" | custom-call | tf_op jit(solution)/shard_map/pivot_gram/pallas_call | solution.py:68
  417.6 0.0 copy-start.2
  417.6 81.0 %solve_update.1 = (f32[4,384,640]{2,1,0:T(8,128)}, f32[4,384,384]{2,1,0:T(8,128)}) custom-call(f32[4,384,1024]{2,1,0:T(8,128)} %pivot_gram.1.g_ref), custom_call_target="tpu_custom_call" | custom-call | tf_op jit(solution)/shard_map/solve_update/pallas_call | solution.py:165
  498.6 1.9 collective-permute-start
  500.6 3.6 collective-permute-start.1
  504.2 2.3 collective-permute-start.2
  506.5 10.5 %collective-permute-start.3 = (f32[4,384,384]{2,1,0:T(8,128)}, f32[4,384,384]{2,1,0:T(8,128)}, u32[]{:S(2)}, u32[]{:S(2)}) collective-permute-start(f32[4,384,384]{2,1,0:T(8,128)} %get-tuple-element.5.own_ref), channel_id=1, source_target_pairs={{1,0},{2,1},{3,2},{4,3},{5,4},{6,5},{7,6},{8,7},{9,8},{10,9},{11,1... | collective-permute-start | bytes 7077896 | tf_op jit(solution)/shard_map/ppermute | solution.py:211
  517.0 0.0 copy-done.2
  517.0 0.6 reshape.11.n_ref
  517.6 11.4 %collective-permute-done.a_ref = f32[4,384,384]{2,1,0:T(8,128)S(1)} collective-permute-done((f32[4,384,384]{2,1,0:T(8,128)}, f32[4,384,384]{2,1,0:T(8,128)S(1)}, u32[]{:S(2)}, u32[]{:S(2)}) %collective-permute-start) | collective-permute-done | bytes 2359328 | tf_op jit(solution)/shard_map/ppermute | solution.py:211
  529.0 0.0 copy-start
  529.0 1.9 collective-permute-done.1.b_ref
  530.9 33.6 %collective-permute-done.2.c_ref = f32[4,384,384]{2,1,0:T(8,128)} collective-permute-done((f32[4,384,384]{2,1,0:T(8,128)}, f32[4,384,384]{2,1,0:T(8,128)}, u32[]{:S(2)}, u32[]{:S(2)}) %collective-permute-start.2) | collective-permute-done | bytes 2359328 | tf_op jit(solution)/shard_map/ppermute | solution.py:211
  564.5 2.6 collective-permute-done.3.d_ref
  567.1 0.0 copy-done
  567.1 6.2 %gather_schur.1 = f32[4,384,384]{2,1,0:T(8,128)} custom-call(s32[16]{0:T(128)} %reshape.11.n_ref, f32[4,384,384]{2,1,0:T(8,128)} %get-tuple-element.5.own_ref, f32[4,384,384]{2,1,0:T(8,128)} %copy-done, f32[4,384,384]{2,1,0:T(8,128)} %collective-permute-done.1.b_ref, f32[4,384,384]{2,1,0:T(8,128)} %collective-permute-done.2.c_ref, ...), custom_call_target="tpu_custom_call" | custom-call | tf_op jit(solution)/shard_map/gather_schur/pallas_call | solution.py:193
  (4 shorter events, 0.0 us)
Async XLA Ops:
  14.3 8.5 %copy-start.1 = (s32[4,1024]{1,0:T(4,128)S(1)}, s32[4,1024]{1,0:T(4,128)}, u32[]{:S(2)}) copy-start(s32[4,1024]{1,0:T(4,128)} %param.8) | copy-start | bytes 49156
  14.3 376.7 %all-to-all-start = ((bf16[16,1536,512]{2,1,0:T(8,128)(2,1)}), bf16[16,1536,512]{2,1,0:T(8,128)(2,1)}, u32[]{:S(2)}, u32[]{:S(2)}) async-start(bf16[16,1536,512]{2,1,0:T(8,128)(2,1)} %place_blocks.1), calls=%async_computation | async-start | bytes 50331648 | tf_op jit(solution)/shard_map/all_to_all | solution.py:230
  417.6 99.4 %copy-start.2 = (s32[4,4]{1,0:T(4,128)S(1)}, s32[4,4]{1,0:T(4,128)}, u32[]{:S(2)}) copy-start(s32[4,4]{1,0:T(4,128)} %param.9) | copy-start | bytes 196
  498.6 30.4 %collective-permute-start = (f32[4,384,384]{2,1,0:T(8,128)}, f32[4,384,384]{2,1,0:T(8,128)S(1)}, u32[]{:S(2)}, u32[]{:S(2)}) collective-permute-start(f32[4,384,384]{2,1,0:T(8,128)} %get-tuple-element.5.own_ref), channel_id=1, source_target_pairs={{0,16},{16,32},{32,48},{48,64},{64,80},{80,96},{96,112},{1,17},{17... | collective-permute-start | bytes 7077896 | tf_op jit(solution)/shard_map/ppermute | solution.py:211
  500.6 30.3 %collective-permute-start.1 = (f32[4,384,384]{2,1,0:T(8,128)}, f32[4,384,384]{2,1,0:T(8,128)}, u32[]{:S(2)}, u32[]{:S(2)}) collective-permute-start(f32[4,384,384]{2,1,0:T(8,128)} %get-tuple-element.5.own_ref), channel_id=1, source_target_pairs={{16,0},{32,16},{48,32},{64,48},{80,64},{96,80},{112,96},{17,1},{33... | collective-permute-start | bytes 7077896 | tf_op jit(solution)/shard_map/ppermute | solution.py:211
  504.2 60.3 %collective-permute-start.2 = (f32[4,384,384]{2,1,0:T(8,128)}, f32[4,384,384]{2,1,0:T(8,128)}, u32[]{:S(2)}, u32[]{:S(2)}) collective-permute-start(f32[4,384,384]{2,1,0:T(8,128)} %get-tuple-element.5.own_ref), channel_id=1, source_target_pairs={{0,1},{1,2},{2,3},{3,4},{4,5},{5,6},{6,7},{7,8},{8,9},{9,10},{10,1... | collective-permute-start | bytes 7077896 | tf_op jit(solution)/shard_map/ppermute | solution.py:211
  506.5 60.7 %collective-permute-start.3 = (f32[4,384,384]{2,1,0:T(8,128)}, f32[4,384,384]{2,1,0:T(8,128)}, u32[]{:S(2)}, u32[]{:S(2)}) collective-permute-start(f32[4,384,384]{2,1,0:T(8,128)} %get-tuple-element.5.own_ref), channel_id=1, source_target_pairs={{1,0},{2,1},{3,2},{4,3},{5,4},{6,5},{7,6},{8,7},{9,8},{10,9},{11,1... | collective-permute-start | bytes 7077896 | tf_op jit(solution)/shard_map/ppermute | solution.py:211
  529.0 38.1 %copy-start = (f32[4,384,384]{2,1,0:T(8,128)}, f32[4,384,384]{2,1,0:T(8,128)S(1)}, u32[]{:S(2)}) copy-start(f32[4,384,384]{2,1,0:T(8,128)S(1)} %collective-permute-done.a_ref) | copy-start | bytes 7077892

commit v2 on v1

--- a/solution.py
+++ b/solution.py
@@ -37,50 +37,111 @@
     )(target, widths, fine_blocks)
 
 
-def gram_kernel(first_ref, second_ref, a_ref, b_ref, piv_ref, o_ref, hot_ref):
-    r = pl.program_id(1)
-    half = a_ref.shape[2]
-
-    @pl.when(r == 0)
-    def _():
-        hot_ref[...] = jnp.where(iota(hot_ref.shape, 0) == piv_ref[0], 1.0, 0.0).astype(hot_ref.dtype)
-
-    pivoted = jnp.dot(a_ref[0], hot_ref[:half, :], preferred_element_type=jnp.float32)
-    pivoted += jnp.dot(b_ref[0], hot_ref[half:, :], preferred_element_type=jnp.float32)
-    pivoted = pivoted.astype(jnp.bfloat16)
-    part = lax.dot_general(
-        pivoted[:, :K], pivoted, (((0,), (0,)), ((), ())), preferred_element_type=jnp.float32
-    )
-
-    @pl.when(r == 0)
-    def _():
-        o_ref[0] = part
-
-    @pl.when(r > 0)
-    def _():
-        o_ref[0] += part
-
-
-def gram_of(arrived, first, second, pivots):
-    peers, rows, half = arrived.shape
+GROUPS, PIECES = 6, 4
+
+
+def exchange_gram_kernel(sel_ref, x_ref, piv_ref, o_ref, hot_ref, send_sem, recv_sems, own_sems, *lands):
+    me = lax.axis_index("yz")
+    plane = lax.axis_size("yz")
+    side = 4
+    clusters, kept, width = o_ref.shape
+    peers, height, half = lands[0].shape
+    step = height // PIECES
+
+    def peer(d):
+        return lax.rem(me // side + d // side, plane // side) * side + lax.rem(me + d, side)
+
+    barrier = pltpu.get_barrier_semaphore()
+
+    def greet(d, carry):
+        pl.semaphore_signal(
+            barrier, inc=1, device_id={"yz": peer(d)}, device_id_type=pl.DeviceIdType.MESH
+        )
+        return carry
+
+    lax.fori_loop(1, peers, greet, 0)
+    pl.semaphore_wait(barrier, peers - 1)
+
+    def own_copy(group):
+        rows = pl.ds(group * height, height)
+        return pltpu.make_async_copy(x_ref.at[me, rows], lands[group].at[me], own_sems.at[group])
+
+    def launch(group):
+        def one(n, carry):
+            piece, to = n // (peers - 1), peer(1 + lax.rem(n, peers - 1))
+            pltpu.make_async_remote_copy(
+                src_ref=x_ref.at[to, pl.ds(pl.multiple_of(group * height + piece * step, step), step)],
+                dst_ref=lands[group].at[me, pl.ds(pl.multiple_of(piece * step, step), step)],
+                send_sem=send_sem,
+                recv_sem=recv_sems.at[group],
+                device_id={"yz": to},
+                device_id_type=pl.DeviceIdType.MESH,
+            ).start()
+            return carry
+
+        lax.fori_loop(0, PIECES * (peers - 1), one, 0)
+        own_copy(group).start()
+
+    launch(0)
+    launch(1)
+
+    def make_hot(c, carry):
+        hot_ref[c] = jnp.where(iota((width, width), 0) == piv_ref[c], 1.0, 0.0).astype(hot_ref.dtype)
+        return carry
+
+    lax.fori_loop(0, clusters, make_hot, 0)
+
+    for group in range(GROUPS):
+        land = lands[group]
+        rest = land.at[pl.ds(0, peers - 1)]
+        pltpu.make_async_copy(rest, rest, recv_sems.at[group]).wait()
+        own_copy(group).wait()
+        if group + 2 < GROUPS:
+            launch(group + 2)
+
+        def one_cluster(c, carry):
+            a, b = land[sel_ref[0, c]], land[sel_ref[1, c]]
+            pivoted = jnp.dot(a, hot_ref[c, :half, :], preferred_element_type=jnp.float32)
+            pivoted += jnp.dot(b, hot_ref[c, half:, :], preferred_element_type=jnp.float32)
+            pivoted = pivoted.astype(jnp.bfloat16)
+            part = lax.dot_general(
+                pivoted[:, :kept], pivoted, (((0,), (0,)), ((), ())), preferred_element_type=jnp.float32
+            )
+            o_ref[c] = part if group == 0 else o_ref[c] + part
+            return carry
+
+        lax.fori_loop(0, clusters, one_cluster, 0)
+
+    whole = x_ref.at[pl.ds(0, peers - 1)]
+    pltpu.make_async_copy(whole, whole, send_sem).wait()
+
+
+def exchange_gram(placed, chosen, pivots):
+    peers, rows, half = placed.shape
     clusters, width = pivots.shape
-    step = 512
+    height = rows // GROUPS
+    vmem = pl.BlockSpec(memory_space=pltpu.VMEM)
     return pl.pallas_call(
-        gram_kernel,
+        exchange_gram_kernel,
         out_shape=jax.ShapeDtypeStruct((clusters, K, width), jnp.float32),
-        grid_spec=pltpu.PrefetchScalarGridSpec(
-            num_scalar_prefetch=2,
-            grid=(clusters, rows // step),
-            in_specs=[
-                pl.BlockSpec((1, step, half), lambda c, r, f, s: (f[c], r, 0)),
-                pl.BlockSpec((1, step, half), lambda c, r, f, s: (s[c], r, 0)),
-                pl.BlockSpec((1, 1, width), lambda c, r, f, s: (c, 0, 0)),
-            ],
-            out_specs=pl.BlockSpec((1, K, width), lambda c, r, f, s: (c, 0, 0)),
-            scratch_shapes=[pltpu.VMEM((width, width), jnp.bfloat16)],
+        in_specs=[
+            pl.BlockSpec(memory_space=pltpu.SMEM),
+            pl.BlockSpec(memory_space=pltpu.HBM),
+            vmem,
+        ],
+        out_specs=vmem,
+        scratch_shapes=[
+            pltpu.VMEM((clusters, width, width), jnp.bfloat16),
+            pltpu.SemaphoreType.DMA,
+            pltpu.SemaphoreType.DMA((GROUPS,)),
+            pltpu.SemaphoreType.DMA((GROUPS,)),
+        ]
+        + [pltpu.VMEM((peers, height, half), jnp.bfloat16) for _ in range(GROUPS)],
+        compiler_params=pltpu.CompilerParams(
+            collective_id=0, has_side_effects=True, vmem_limit_bytes=58 * 1024 * 1024
         ),
-        name="pivot_gram",
-    )(first, second, arrived, arrived, pivots[:, None, :])
+        name="exchange_gram",
+    )(chosen, placed, pivots[:, None, :])
 
 
 def packed_inverse(s):
@@ -227,8 +288,7 @@
     first = jnp.min(jnp.where(mine, peer, yz_count - 1), axis=(1, 2))
     second = jnp.max(jnp.where(mine, peer, 0), axis=(1, 2))
     placed = place_blocks(fine_blocks, target, widths, yz_count)
-    arrived = lax.all_to_all(placed, "yz", split_axis=0, concat_axis=0, tiled=True)
-    interp, update = solve(gram_of(arrived, first, second, pivots))
+    interp, update = solve(exchange_gram(placed, jnp.stack([first, second]), pivots))
     return interp, gather_schur(update, from_sides(update), neighbours)
 
 

time: 577 us -> 461 us (0.80)
  waiting for transfers between devices: 416 us -> 51.4 us
  Pallas kernels: 126 us -> 388 us
  starting transfers between devices: 26.9 us -> 12.8 us
    all_to_all x1 -> x0, waiting for transfers between devices: 367 us -> none  [body(): lax.all_to_all(placed, 'yz', split_axis=0, concat_axis=0, tiled=True)]
    pallas_call x1, Pallas kernels: 26.7 us -> 288 us  [exchange_gram(): pl.pallas_call(exchange_gram_kernel, out_shape=jax.ShapeDtypeStruct((clus...]
    all_to_all x1 -> x0, starting transfers between devices: 8.54 us -> none  [body(): lax.all_to_all(placed, 'yz', split_axis=0, concat_axis=0, tiled=True)]
    ppermute x2, starting transfers between devices: 14.2 us -> 7.51 us  [from_sides(): lax.ppermute(x, axis, [(b, a) for a, b in up])]
  transfers between devices with their start and end apart: 5 -> 4, of which waited for: 5 -> 4; matrix products, arithmetic and copies ran while one was open for 0% -> 0% of each run, Pallas kernels for 0% -> 0%
where the time goes in v2:
time: 461 us; the launch traced here: 457 us
  Pallas kernels  388 us (84%)
  waiting for transfers between devices  51.4 us (11%)
  starting transfers between devices  12.8 us (3%)
    pallas_call x1, Pallas kernels, exchange_gram(): pl.pallas_call(exchange_gram_kernel, out_shape=jax.ShapeDtypeStruct((clus...  288 us
    pallas_call x1, Pallas kernels, solve(): pl.pallas_call(solve_kernel, out_shape=(jax.ShapeDtypeStruct((clusters, k...  81.2 us
    ppermute x2, waiting for transfers between devices, from_sides(): lax.ppermute(x, axis, up)  46 us
    pallas_call x1, Pallas kernels, place_blocks(): pl.pallas_call(place_kernel, out_shape=jax.ShapeDtypeStruct((peers, rows,...  12 us
  transfers between devices with their start and end apart: 4, of which 4 were waited for; matrix products, arithmetic and copies ran while one was open for 0% of the time, Pallas kernels for 0%

profile of v2, /device:TPU:10, one launch (start us, length us, event | category | flops | bytes accessed | tf_op | source)
XLA Modules:
  0.0 457.3 jit_solution(16821806479306109024)
XLA Ops:
  0.6 0.8 reshape.10
  1.4 0.1 copy.18
  1.5 1.3 broadcast_in_dim.31.piv_ref
  2.9 0.2 select_reduce_fusion.1
  3.1 0.6 pad_add_fusion.sel_ref
  3.7 0.7 dynamic-slice_reduce_fusion.target_ref
  4.4 12.0 %place_blocks.1.x_ref = bf16[16,1536,512]{2,1,0:T(8,128)(2,1)} custom-call(s32[8]{0:T(128)} %dynamic-slice_reduce_fusion.target_ref, s32[8]{0:T(128)} %widths_ref.1, bf16[8,1536,512]{2,1,0:T(8,128)(2,1)} %x_ref.1), custom_call_target="tpu_custom_call" | custom-call | tf_op jit(solution)/shard_map/place_blocks/pallas_call | solution.py:27
  16.4 288.5 %exchange_gram.1.g_ref = f32[4,384,1024]{2,1,0:T(8,128)} custom-call(s32[2,4]{1,0:T(2,128)} %pad_add_fusion.sel_ref, bf16[16,1536,512]{2,1,0:T(8,128)(2,1)} %place_blocks.1.x_ref, s32[4,1,1024]{2,1,0:T(1,128)} %broadcast_in_dim.31.piv_ref), custom_call_target="tpu_custom_call" | custom-call | tf_op jit(solution)/shard_map/exchange_gram/pallas_call | solution.py:124
  304.9 0.0 copy-start.1
  304.9 81.2 %solve_update.1 = (f32[4,384,640]{2,1,0:T(8,128)}, f32[4,384,384]{2,1,0:T(8,128)}) custom-call(f32[4,384,1024]{2,1,0:T(8,128)} %exchange_gram.1.g_ref), custom_call_target="tpu_custom_call" | custom-call | tf_op jit(solution)/shard_map/solve_update/pallas_call | solution.py:226
  386.1 1.9 collective-permute-start
  388.0 3.6 collective-permute-start.1
  391.7 3.4 collective-permute-start.2
  395.1 3.9 collective-permute-start.3
  399.0 0.0 copy-done.1
  399.0 0.7 reshape.11.n_ref
  399.7 16.8 %collective-permute-done.a_ref = f32[4,384,384]{2,1,0:T(8,128)S(1)} collective-permute-done((f32[4,384,384]{2,1,0:T(8,128)}, f32[4,384,384]{2,1,0:T(8,128)S(1)}, u32[]{:S(2)}, u32[]{:S(2)}) %collective-permute-start) | collective-permute-done | bytes 2359328 | tf_op jit(solution)/shard_map/ppermute | solution.py:272
  416.5 0.0 copy-start
  416.5 1.9 collective-permute-done.1.b_ref
  418.3 29.2 %collective-permute-done.2.c_ref = f32[4,384,384]{2,1,0:T(8,128)} collective-permute-done((f32[4,384,384]{2,1,0:T(8,128)}, f32[4,384,384]{2,1,0:T(8,128)}, u32[]{:S(2)}, u32[]{:S(2)}) %collective-permute-start.2) | collective-permute-done | bytes 2359328 | tf_op jit(solution)/shard_map/ppermute | solution.py:272
  447.5 3.5 collective-permute-done.3.d_ref
  451.1 0.0 copy-done
  451.1 6.2 %gather_schur.1 = f32[4,384,384]{2,1,0:T(8,128)} custom-call(s32[16]{0:T(128)} %reshape.11.n_ref, f32[4,384,384]{2,1,0:T(8,128)} %get-tuple-element.5.own_ref, f32[4,384,384]{2,1,0:T(8,128)} %copy-done, f32[4,384,384]{2,1,0:T(8,128)} %collective-permute-done.1.b_ref, f32[4,384,384]{2,1,0:T(8,128)} %collective-permute-done.2.c_ref, ...), custom_call_target="tpu_custom_call" | custom-call | tf_op jit(solution)/shard_map/gather_schur/pallas_call | solution.py:254
  (4 shorter events, 0.0 us)
Async XLA Ops:
  304.9 94.1 %copy-start.1 = (s32[4,4]{1,0:T(4,128)S(1)}, s32[4,4]{1,0:T(4,128)}, u32[]{:S(2)}) copy-start(s32[4,4]{1,0:T(4,128)} %param.9) | copy-start | bytes 196
  386.1 30.4 %collective-permute-start = (f32[4,384,384]{2,1,0:T(8,128)}, f32[4,384,384]{2,1,0:T(8,128)S(1)}, u32[]{:S(2)}, u32[]{:S(2)}) collective-permute-start(f32[4,384,384]{2,1,0:T(8,128)} %get-tuple-element.5.own_ref), channel_id=1, source_target_pairs={{0,16},{16,32},{32,48},{48,64},{64,80},{80,96},{96,112},{1,17},{17... | collective-permute-start | bytes 7077896 | tf_op jit(solution)/shard_map/ppermute | solution.py:272
  388.0 30.3 %collective-permute-start.1 = (f32[4,384,384]{2,1,0:T(8,128)}, f32[4,384,384]{2,1,0:T(8,128)}, u32[]{:S(2)}, u32[]{:S(2)}) collective-permute-start(f32[4,384,384]{2,1,0:T(8,128)} %get-tuple-element.5.own_ref), channel_id=1, source_target_pairs={{16,0},{32,16},{48,32},{64,48},{80,64},{96,80},{112,96},{17,1},{33... | collective-permute-start | bytes 7077896 | tf_op jit(solution)/shard_map/ppermute | solution.py:272
  391.7 55.9 %collective-permute-start.2 = (f32[4,384,384]{2,1,0:T(8,128)}, f32[4,384,384]{2,1,0:T(8,128)}, u32[]{:S(2)}, u32[]{:S(2)}) collective-permute-start(f32[4,384,384]{2,1,0:T(8,128)} %get-tuple-element.5.own_ref), channel_id=1, source_target_pairs={{0,1},{1,2},{2,3},{3,4},{4,5},{5,6},{6,7},{7,8},{8,9},{9,10},{10,1... | collective-permute-start | bytes 7077896 | tf_op jit(solution)/shard_map/ppermute | solution.py:272
  395.1 55.9 %collective-permute-start.3 = (f32[4,384,384]{2,1,0:T(8,128)}, f32[4,384,384]{2,1,0:T(8,128)}, u32[]{:S(2)}, u32[]{:S(2)}) collective-permute-start(f32[4,384,384]{2,1,0:T(8,128)} %get-tuple-element.5.own_ref), channel_id=1, source_target_pairs={{1,0},{2,1},{3,2},{4,3},{5,4},{6,5},{7,6},{8,7},{9,8},{10,9},{11,1... | collective-permute-start | bytes 7077896 | tf_op jit(solution)/shard_map/ppermute | solution.py:272
  416.5 34.6 %copy-start = (f32[4,384,384]{2,1,0:T(8,128)}, f32[4,384,384]{2,1,0:T(8,128)S(1)}, u32[]{:S(2)}) copy-start(f32[4,384,384]{2,1,0:T(8,128)S(1)} %collective-permute-done.a_ref) | copy-start | bytes 7077892

commit v3 on v2

--- a/solution.py
+++ b/solution.py
@@ -145,16 +145,41 @@
 
 
 def packed_inverse(s):
-    lane, row = iota(s.shape, 1), iota(s.shape, 0)
+    lane, row = iota((8, 128), 1), iota((8, 128), 0)
     inner = lane % 32
     base = lane - inner
-    for k in range(32):
-        col = jnp.take_along_axis(s, base + k, axis=1)
-        here = inner == k
-        scale = 1.0 / jnp.broadcast_to(col[k : k + 1], s.shape)
-        scaled = jnp.where(here, scale, jnp.broadcast_to(s[k : k + 1], s.shape) * scale)
-        s = jnp.where(row == k, scaled, jnp.where(here, 0.0, s) - col * scaled)
-    return s
+    s = [s[8 * t : 8 * t + 8] for t in range(4)]
+
+    def spread(x, k):
+        return jnp.broadcast_to(x[k % 8 : k % 8 + 1], (8, 128))
+
+    for k in range(0, 32, 4):
+        at = k // 8
+        cols = [
+            [jnp.take_along_axis(x, base + (k + j), axis=1, mode="promise_in_bounds") for x in s]
+            for j in range(4)
+        ]
+        here = (inner >= k) & (inner < k + 4)
+        d = [[spread(cols[j][at], k + i) for j in range(4)] for i in range(4)]
+        w = [jnp.where(here, jnp.where(inner == k + i, 1.0, 0.0), spread(s[at], k + i)) for i in range(4)]
+        for p in range(4):
+            scale = 1.0 / d[p][p]
+            w[p] = w[p] * scale
+            for j in range(p + 1, 4):
+                d[p][j] = d[p][j] * scale
+            for i in range(4):
+                if i != p:
+                    w[i] = w[i] - d[i][p] * w[p]
+                    for j in range(p + 1, 4):
+                        d[i][j] = d[i][j] - d[i][p] * d[p][j]
+        for t in range(4):
+            x = jnp.where(here, 0.0, s[t])
+            x = x - (cols[0][t] * w[0] + cols[1][t] * w[1]) - (cols[2][t] * w[2] + cols[3][t] * w[3])
+            if t == at:
+                for i in range(4):
+                    x = jnp.where(row == (k + i) % 8, w[i], x)
+            s[t] = x
+    return jnp.concatenate(s, axis=0)
 
 
 def invert_diagonal(d_ref):
@@ -185,6 +210,26 @@
             d_ref[c] = kept + jnp.dot(lhs, full, precision=HIGH, preferred_element_type=jnp.float32)
 
 
+def split3(x):
+    a = x.astype(jnp.bfloat16)
+    x = x - a.astype(jnp.float32)
+    b = x.astype(jnp.bfloat16)
+    return a, b, (x - b.astype(jnp.float32)).astype(jnp.bfloat16)
+
+
+def lhs_terms(x):
+    a, b, c = split3(x)
+    return jnp.concatenate([a, a, b, a, c, b], axis=1)
+
+
+def rhs_terms(x):
+    a, b, c = split3(x)
+    return jnp.concatenate([a, b, a, c, a, b], axis=0)
+
+
+LOWER = ((0, 0), (1, 0), (1, 1), (2, 0), (2, 1), (2, 2))
+
+
 def solve_kernel(g_ref, interp_ref, update_ref, w_ref, d_ref):
     clusters, width = g_ref.shape[0], g_ref.shape[2]
     w_ref[...] = g_ref[...]
@@ -196,13 +241,16 @@
         invert_diagonal(d_ref)
 
         def one(c, carry):
-            scaled = jnp.dot(d_ref[c], w_ref[c, at, :], precision=HIGH, preferred_element_type=jnp.float32)
+            scaled = jnp.dot(
+                lhs_terms(d_ref[c]), rhs_terms(w_ref[c, at, :]), preferred_element_type=jnp.float32
+            )
             w_ref[c, at, :] = scaled
+            terms = rhs_terms(scaled)
             for far in range(1, K // 128):
                 other = lax.rem(s + far, K // 128)
                 rows = pl.ds(pl.multiple_of(other * 128, 128), 128)
                 w_ref[c, rows, :] = w_ref[c, rows, :] - jnp.dot(
-                    w_ref[c, rows, at], scaled, precision=HIGH, preferred_element_type=jnp.float32
+                    lhs_terms(w_ref[c, rows, at]), terms, preferred_element_type=jnp.float32
                 )
             return carry
 
@@ -213,9 +261,14 @@
     def finish(c, carry):
         x = w_ref[c, :, K:]
         interp_ref[c] = x
-        update_ref[c] = lax.dot_general(
-            x, x, (((1,), (1,)), ((), ())), precision=HIGH, preferred_element_type=jnp.float32
-        )
+        a, b, _ = split3(x)
+        lhs = jnp.concatenate([a, a, b], axis=1)
+        rhs = jnp.concatenate([a, b, a], axis=1)
+        across = (((1,), (1,)), ((), ()))
+        left = lax.dot_general(lhs, rhs[:256], across, preferred_element_type=jnp.float32)
+        last = lax.dot_general(lhs[256:], rhs[256:], across, preferred_element_type=jnp.float32)
+        for n, (i, j) in enumerate(LOWER):
+            update_ref[c, n] = last if j == 2 else left[128 * i : 128 * i + 128, 128 * j : 128 * j + 128]
         return carry
 
     lax.fori_loop(0, clusters, finish, 0)
@@ -223,14 +276,15 @@
 
 def solve(gram):
     clusters, kept, width = gram.shape
+    vmem = pl.BlockSpec(memory_space=pltpu.VMEM)
     return pl.pallas_call(
         solve_kernel,
         out_shape=(
             jax.ShapeDtypeStruct((clusters, kept, width - kept), jnp.float32),
-            jax.ShapeDtypeStruct((clusters, kept, kept), jnp.float32),
+            jax.ShapeDtypeStruct((clusters, len(LOWER), 128, 128), jnp.float32),
         ),
-        in_specs=[pl.BlockSpec(memory_space=pltpu.VMEM)],
-        out_specs=(pl.BlockSpec(memory_space=pltpu.VMEM), pl.BlockSpec(memory_space=pltpu.VMEM)),
+        in_specs=[vmem],
+        out_specs=(vmem, vmem),
         scratch_shapes=[
             pltpu.VMEM((clusters, kept, width), jnp.float32),
             pltpu.VMEM((clusters, 128, 128), jnp.float32),
@@ -241,24 +295,28 @@
 
 
 def schur_kernel(n_ref, own_ref, a_ref, b_ref, c_ref, d_ref, o_ref):
-    o_ref[...] = own_ref[...] + ((a_ref[...] + b_ref[...]) + (c_ref[...] + d_ref[...]))
+    for n, (i, j) in enumerate(LOWER):
+        x = own_ref[0, n] + ((a_ref[0, n] + b_ref[0, n]) + (c_ref[0, n] + d_ref[0, n]))
+        o_ref[0, 128 * i : 128 * i + 128, 128 * j : 128 * j + 128] = x
+        if i != j:
+            o_ref[0, 128 * j : 128 * j + 128, 128 * i : 128 * i + 128] = x.T
 
 
 def gather_schur(update, sides, neighbours):
-    clusters, kept, _ = update.shape
+    clusters = update.shape[0]
+    block = (1,) + update.shape[1:]
 
     def pick(side):
-        return pl.BlockSpec((1, kept, kept), lambda c, n: (n[4 * c + side], 0, 0))
-
-    own = pl.BlockSpec((1, kept, kept), lambda c, n: (c, 0, 0))
+        return pl.BlockSpec(block, lambda c, n: (n[4 * c + side], 0, 0, 0))
+
     return pl.pallas_call(
         schur_kernel,
-        out_shape=jax.ShapeDtypeStruct(update.shape, jnp.float32),
+        out_shape=jax.ShapeDtypeStruct((clusters, K, K), jnp.float32),
         grid_spec=pltpu.PrefetchScalarGridSpec(
             num_scalar_prefetch=1,
             grid=(clusters,),
-            in_specs=[own] + [pick(side) for side in range(4)],
-            out_specs=own,
+            in_specs=[pl.BlockSpec(block, lambda c, n: (c, 0, 0, 0))] + [pick(side) for side in range(4)],
+            out_specs=pl.BlockSpec((1, K, K), lambda c, n: (c, 0, 0)),
         ),
         name="gather_schur",
     )(neighbours.reshape(-1), update, *sides)

time: 461 us -> 415 us (0.900)
  Pallas kernels: 388 us -> 358 us
  waiting for transfers between devices: 51.4 us -> 34.8 us
    pallas_call x1, Pallas kernels: 81.2 us -> 51.2 us  [solve(): pl.pallas_call(solve_kernel, out_shape=(jax.ShapeDtypeStruct((clusters, k...]
    ppermute x2, waiting for transfers between devices: 46 us -> 29 us  [from_sides(): lax.ppermute(x, axis, up)]
where the time goes in v3:
time: 415 us; the launch traced here: 412 us
  Pallas kernels  358 us (86%)
  waiting for transfers between devices  34.8 us (8%)
  starting transfers between devices  13.7 us (3%)
    pallas_call x1, Pallas kernels, exchange_gram(): pl.pallas_call(exchange_gram_kernel, out_shape=jax.ShapeDtypeStruct((clus...  289 us
    pallas_call x1, Pallas kernels, solve(): pl.pallas_call(solve_kernel, out_shape=(jax.ShapeDtypeStruct((clusters, k...  51.2 us
    ppermute x2, waiting for transfers between devices, from_sides(): lax.ppermute(x, axis, up)  29 us
    pallas_call x1, Pallas kernels, place_blocks(): pl.pallas_call(place_kernel, out_shape=jax.ShapeDtypeStruct((peers, rows,...  12.1 us
  transfers between devices with their start and end apart: 4, of which 4 were waited for; matrix products, arithmetic and copies ran while one was open for 0% of the time, Pallas kernels for 0%

profile of v3, /device:TPU:10, one launch (start us, length us, event | category | flops | bytes accessed | tf_op | source)
XLA Modules:
  0.0 411.8 jit_solution(10817039479617148555)
XLA Ops:
  0.6 0.8 reshape.10
  1.4 0.1 copy.18
  1.5 1.3 broadcast_in_dim.31.piv_ref
  2.9 0.2 select_reduce_fusion.1
  3.1 0.6 pad_add_fusion.sel_ref
  3.7 0.7 dynamic-slice_reduce_fusion.target_ref
  4.4 12.1 %place_blocks.1.x_ref = bf16[16,1536,512]{2,1,0:T(8,128)(2,1)} custom-call(s32[8]{0:T(128)} %dynamic-slice_reduce_fusion.target_ref, s32[8]{0:T(128)} %widths_ref.1, bf16[8,1536,512]{2,1,0:T(8,128)(2,1)} %x_ref.1), custom_call_target="tpu_custom_call" | custom-call | tf_op jit(solution)/shard_map/place_blocks/pallas_call | solution.py:27
  16.5 289.4 %exchange_gram.1.g_ref = f32[4,384,1024]{2,1,0:T(8,128)} custom-call(s32[2,4]{1,0:T(2,128)} %pad_add_fusion.sel_ref, bf16[16,1536,512]{2,1,0:T(8,128)(2,1)} %place_blocks.1.x_ref, s32[4,1,1024]{2,1,0:T(1,128)} %broadcast_in_dim.31.piv_ref), custom_call_target="tpu_custom_call" | custom-call | tf_op jit(solution)/shard_map/exchange_gram/pallas_call | solution.py:124
  305.9 0.0 copy-start.2
  305.9 51.2 %solve_update.1 = (f32[4,384,640]{2,1,0:T(8,128)}, f32[4,6,128,128]{3,2,1,0:T(8,128)}) custom-call(f32[4,384,1024]{2,1,0:T(8,128)} %exchange_gram.1.g_ref), custom_call_target="tpu_custom_call" | custom-call | tf_op jit(solution)/shard_map/solve_update/pallas_call | solution.py:280
  357.1 1.9 collective-permute-start
  359.0 3.6 collective-permute-start.1
  362.7 4.1 collective-permute-start.2
  366.7 4.1 collective-permute-start.3
  370.9 0.0 copy-done.2
  370.9 0.6 reshape.11.n_ref
  371.5 7.5 %collective-permute-done.a_ref = f32[4,6,128,128]{3,2,1,0:T(8,128)S(1)} collective-permute-done((f32[4,6,128,128]{3,2,1,0:T(8,128)}, f32[4,6,128,128]{3,2,1,0:T(8,128)S(1)}, u32[]{:S(2)}, u32[]{:S(2)}) %collective-permute-start) | collective-permute-done | bytes 1572896 | tf_op jit(solution)/shard_map/ppermute | solution.py:330
  379.0 0.0 copy-start
  379.0 1.9 collective-permute-done.1.b_ref
  380.9 0.0 copy-start.1
  380.9 21.5 %collective-permute-done.2.c_ref = f32[4,6,128,128]{3,2,1,0:T(8,128)} collective-permute-done((f32[4,6,128,128]{3,2,1,0:T(8,128)}, f32[4,6,128,128]{3,2,1,0:T(8,128)}, u32[]{:S(2)}, u32[]{:S(2)}) %collective-permute-start.2) | collective-permute-done | bytes 1572896 | tf_op jit(solution)/shard_map/ppermute | solution.py:330
  402.4 3.9 collective-permute-done.3.d_ref
  406.3 0.0 copy-done
  406.3 0.0 copy-done.1
  406.3 5.5 %gather_schur.1 = f32[4,384,384]{2,1,0:T(8,128)} custom-call(s32[16]{0:T(128)} %reshape.11.n_ref, f32[4,6,128,128]{3,2,1,0:T(8,128)} %get-tuple-element.5.own_ref, f32[4,6,128,128]{3,2,1,0:T(8,128)} %copy-done, f32[4,6,128,128]{3,2,1,0:T(8,128)} %copy-done.1, f32[4,6,128,128]{3,2,1,0:T(8,128)} %collective-permute-done.2.c_ref, ...), custom_call_target="tpu_custom_call" | custom-call | tf_op jit(solution)/shard_map/gather_schur/pallas_call | solution.py:312
  (4 shorter events, 0.0 us)
Async XLA Ops:
  305.9 65.0 %copy-start.2 = (s32[4,4]{1,0:T(4,128)S(1)}, s32[4,4]{1,0:T(4,128)}, u32[]{:S(2)}) copy-start(s32[4,4]{1,0:T(4,128)} %param.9) | copy-start | bytes 196
  357.1 21.9 %collective-permute-start = (f32[4,6,128,128]{3,2,1,0:T(8,128)}, f32[4,6,128,128]{3,2,1,0:T(8,128)S(1)}, u32[]{:S(2)}, u32[]{:S(2)}) collective-permute-start(f32[4,6,128,128]{3,2,1,0:T(8,128)} %get-tuple-element.5.own_ref), channel_id=1, source_target_pairs={{0,16},{16,32},{32,48},{48,64},{64,80},{80,96},{96,112},{1,17},{17... | collective-permute-start | bytes 4718600 | tf_op jit(solution)/shard_map/ppermute | solution.py:330
  359.0 21.9 %collective-permute-start.1 = (f32[4,6,128,128]{3,2,1,0:T(8,128)}, f32[4,6,128,128]{3,2,1,0:T(8,128)S(1)}, u32[]{:S(2)}, u32[]{:S(2)}) collective-permute-start(f32[4,6,128,128]{3,2,1,0:T(8,128)} %get-tuple-element.5.own_ref), channel_id=1, source_target_pairs={{16,0},{32,16},{48,32},{64,48},{80,64},{96,80},{112,96},{17,1},{33... | collective-permute-start | bytes 4718600 | tf_op jit(solution)/shard_map/ppermute | solution.py:330
  362.7 39.7 %collective-permute-start.2 = (f32[4,6,128,128]{3,2,1,0:T(8,128)}, f32[4,6,128,128]{3,2,1,0:T(8,128)}, u32[]{:S(2)}, u32[]{:S(2)}) collective-permute-start(f32[4,6,128,128]{3,2,1,0:T(8,128)} %get-tuple-element.5.own_ref), channel_id=1, source_target_pairs={{0,1},{1,2},{2,3},{3,4},{4,5},{5,6},{6,7},{7,8},{8,9},{9,10},{10,1... | collective-permute-start | bytes 4718600 | tf_op jit(solution)/shard_map/ppermute | solution.py:330
  366.7 39.5 %collective-permute-start.3 = (f32[4,6,128,128]{3,2,1,0:T(8,128)}, f32[4,6,128,128]{3,2,1,0:T(8,128)}, u32[]{:S(2)}, u32[]{:S(2)}) collective-permute-start(f32[4,6,128,128]{3,2,1,0:T(8,128)} %get-tuple-element.5.own_ref), channel_id=1, source_target_pairs={{1,0},{2,1},{3,2},{4,3},{5,4},{6,5},{7,6},{8,7},{9,8},{10,9},{11,1... | collective-permute-start | bytes 4718600 | tf_op jit(solution)/shard_map/ppermute | solution.py:330
  379.0 27.3 %copy-start = (f32[4,6,128,128]{3,2,1,0:T(8,128)}, f32[4,6,128,128]{3,2,1,0:T(8,128)S(1)}, u32[]{:S(2)}) copy-start(f32[4,6,128,128]{3,2,1,0:T(8,128)S(1)} %collective-permute-done.a_ref) | copy-start | bytes 4718596
  380.9 25.4 %copy-start.1 = (f32[4,6,128,128]{3,2,1,0:T(8,128)}, f32[4,6,128,128]{3,2,1,0:T(8,128)S(1)}, u32[]{:S(2)}) copy-start(f32[4,6,128,128]{3,2,1,0:T(8,128)S(1)} %collective-permute-done.1.b_ref) | copy-start | bytes 4718596

commit v4 on v3

--- a/solution.py
+++ b/solution.py
@@ -15,32 +15,13 @@
     return lax.broadcasted_iota(jnp.int32, shape, dim)
 
 
-def place_kernel(target_ref, widths_ref, x_ref, o_ref):
-    b = pl.program_id(0)
-    x = x_ref[0]
-    live = iota(x.shape, 1) < widths_ref[b]
-    o_ref[0] = jnp.where(live, x, jnp.zeros_like(x))
-
-
-def place_blocks(fine_blocks, target, widths, peers):
-    count, rows, cols = fine_blocks.shape
-    return pl.pallas_call(
-        place_kernel,
-        out_shape=jax.ShapeDtypeStruct((peers, rows, cols), fine_blocks.dtype),
-        grid_spec=pltpu.PrefetchScalarGridSpec(
-            num_scalar_prefetch=2,
-            grid=(count,),
-            in_specs=[pl.BlockSpec((1, rows, cols), lambda b, t, w: (b, 0, 0))],
-            out_specs=pl.BlockSpec((1, rows, cols), lambda b, t, w: (t[b], 0, 0)),
-        ),
-        name="place_blocks",
-    )(target, widths, fine_blocks)
-
-
-GROUPS, PIECES = 6, 4
-
-
-def exchange_gram_kernel(sel_ref, x_ref, piv_ref, o_ref, hot_ref, send_sem, recv_sems, own_sems, *lands):
+GROUPS, PIECES, STAGES = 6, 4, 3
+
+
+def exchange_gram_kernel(
+    sel_ref, slot_ref, x_ref, piv_ref, o_ref, hot_ref, send_sems, recv_sems, in_sems, *bufs
+):
+    lands, slots, blocks = bufs[:GROUPS], bufs[GROUPS : GROUPS + STAGES], bufs[GROUPS + STAGES :]
     me = lax.axis_index("yz")
     plane = lax.axis_size("yz")
     side = 4
@@ -51,6 +32,13 @@
     def peer(d):
         return lax.rem(me // side + d // side, plane // side) * side + lax.rem(me + d, side)
 
+    def fetch(group):
+        return pltpu.make_async_copy(
+            x_ref.at[:, pl.ds(group * height, height)], blocks[group % 2], in_sems.at[group % 2]
+        )
+
+    fetch(0).start()
+    fetch(1).start()
     barrier = pltpu.get_barrier_semaphore()
 
     def greet(d, carry):
@@ -60,19 +48,38 @@
         return carry
 
     lax.fori_loop(1, peers, greet, 0)
-    pl.semaphore_wait(barrier, peers - 1)
-
-    def own_copy(group):
-        rows = pl.ds(group * height, height)
-        return pltpu.make_async_copy(x_ref.at[me, rows], lands[group].at[me], own_sems.at[group])
+
+    def sent(group):
+        rest = slots[group % STAGES].at[pl.ds(0, peers - 1)]
+        pltpu.make_async_copy(rest, rest, send_sems.at[group % STAGES]).wait()
+
+    def fill(group):
+        fetch(group).wait()
+        if group >= STAGES:
+            sent(group - STAGES)
+        column = iota((height, half), 1)
+
+        def masked(t):
+            x = blocks[group % 2][slot_ref[0, t]]
+            return jnp.where(column < slot_ref[1, t], x, jnp.zeros_like(x))
+
+        def one(d, carry):
+            slots[group % STAGES][peer(d)] = masked(peer(d))
+            return carry
+
+        lax.fori_loop(1, peers, one, 0)
+        lands[group][me] = masked(me)
+        if group + 2 < GROUPS:
+            fetch(group + 2).start()
 
     def launch(group):
         def one(n, carry):
             piece, to = n // (peers - 1), peer(1 + lax.rem(n, peers - 1))
+            rows = pl.ds(pl.multiple_of(piece * step, step), step)
             pltpu.make_async_remote_copy(
-                src_ref=x_ref.at[to, pl.ds(pl.multiple_of(group * height + piece * step, step), step)],
-                dst_ref=lands[group].at[me, pl.ds(pl.multiple_of(piece * step, step), step)],
-                send_sem=send_sem,
+                src_ref=slots[group % STAGES].at[to, rows],
+                dst_ref=lands[group].at[me, rows],
+                send_sem=send_sems.at[group % STAGES],
                 recv_sem=recv_sems.at[group],
                 device_id={"yz": to},
                 device_id_type=pl.DeviceIdType.MESH,
@@ -80,9 +87,11 @@
             return carry
 
         lax.fori_loop(0, PIECES * (peers - 1), one, 0)
-        own_copy(group).start()
-
+
+    fill(0)
+    pl.semaphore_wait(barrier, peers - 1)
     launch(0)
+    fill(1)
     launch(1)
 
     def make_hot(c, carry):
@@ -90,12 +99,12 @@
         return carry
 
     lax.fori_loop(0, clusters, make_hot, 0)
+    fill(2)
 
     for group in range(GROUPS):
         land = lands[group]
         rest = land.at[pl.ds(0, peers - 1)]
         pltpu.make_async_copy(rest, rest, recv_sems.at[group]).wait()
-        own_copy(group).wait()
         if group + 2 < GROUPS:
             launch(group + 2)
 
@@ -111,37 +120,37 @@
             return carry
 
         lax.fori_loop(0, clusters, one_cluster, 0)
-
-    whole = x_ref.at[pl.ds(0, peers - 1)]
-    pltpu.make_async_copy(whole, whole, send_sem).wait()
-
-
-def exchange_gram(placed, chosen, pivots):
-    peers, rows, half = placed.shape
+        if group + STAGES < GROUPS:
+            fill(group + STAGES)
+
+    for group in range(GROUPS - STAGES, GROUPS):
+        sent(group)
+
+
+def exchange_gram(fine_blocks, slots, chosen, pivots):
+    count, rows, half = fine_blocks.shape
+    peers = slots.shape[1]
     clusters, width = pivots.shape
     height = rows // GROUPS
-    vmem = pl.BlockSpec(memory_space=pltpu.VMEM)
+    vmem, smem = pl.BlockSpec(memory_space=pltpu.VMEM), pl.BlockSpec(memory_space=pltpu.SMEM)
     return pl.pallas_call(
         exchange_gram_kernel,
         out_shape=jax.ShapeDtypeStruct((clusters, K, width), jnp.float32),
-        in_specs=[
-            pl.BlockSpec(memory_space=pltpu.SMEM),
-            pl.BlockSpec(memory_space=pltpu.HBM),
-            vmem,
-        ],
+        in_specs=[smem, smem, pl.BlockSpec(memory_space=pltpu.HBM), vmem],
         out_specs=vmem,
         scratch_shapes=[
             pltpu.VMEM((clusters, width, width), jnp.bfloat16),
-            pltpu.SemaphoreType.DMA,
+            pltpu.SemaphoreType.DMA((STAGES,)),
             pltpu.SemaphoreType.DMA((GROUPS,)),
-            pltpu.SemaphoreType.DMA((GROUPS,)),
+            pltpu.SemaphoreType.DMA((2,)),
         ]
-        + [pltpu.VMEM((peers, height, half), jnp.bfloat16) for _ in range(GROUPS)],
+        + [pltpu.VMEM((peers, height, half), jnp.bfloat16) for _ in range(GROUPS + STAGES)]
+        + [pltpu.VMEM((count, height, half), jnp.bfloat16) for _ in range(2)],
         compiler_params=pltpu.CompilerParams(
-            collective_id=0, has_side_effects=True, vmem_limit_bytes=58 * 1024 * 1024
+            collective_id=0, has_side_effects=True, vmem_limit_bytes=63 * 1024 * 1024
         ),
         name="exchange_gram",
-    )(chosen, placed, pivots[:, None, :])
+    )(chosen, slots, fine_blocks, pivots[:, None, :])
 
 
 def packed_inverse(s):
@@ -182,49 +191,64 @@
     return jnp.concatenate(s, axis=0)
 
 
+def split3(x):
+    a = x.astype(jnp.bfloat16)
+    x = x - a.astype(jnp.float32)
+    b = x.astype(jnp.bfloat16)
+    return a, b, (x - b.astype(jnp.float32)).astype(jnp.bfloat16)
+
+
+def lhs_terms(x):
+    a, b, c = split3(x)
+    return jnp.concatenate([a, a, b, a, c, b], axis=1)
+
+
+def rhs_terms(x):
+    a, b, c = split3(x)
+    return jnp.concatenate([a, b, a, c, a, b], axis=0)
+
+
 def invert_diagonal(d_ref):
-    lane, row = iota((128, 128), 1), iota((128, 128), 0)
+    lane = iota((128, 128), 1)
     lane32 = iota((32, 128), 1)
+    segment = lane32 // 32
+    pad = jnp.zeros((64, 128), jnp.bfloat16)
     for q in range(4):
         lo, hi = 32 * q, 32 * q + 32
         packed = jnp.zeros((32, 128), jnp.float32)
         for c in range(4):
             rows = d_ref[c, lo:hi, :]
             moved = pltpu.roll(rows, (32 * (c - q)) % 128, 1) if c != q else rows
-            packed = jnp.where(lane32 // 32 == c, moved, packed)
+            packed = jnp.where(segment == c, moved, packed)
         packed = packed_inverse(packed)
+        turned = [packed] + [pltpu.roll(packed, 32 * t, 1) for t in range(1, 4)]
         in_cols = (lane >= lo) & (lane < hi)
-        in_rows = (row >= lo) & (row < hi)
-        in_lanes = (lane32 >= lo) & (lane32 < hi)
+        in_lanes = segment == q
         for c in range(4):
-            moved = pltpu.roll(packed, (32 * (q - c)) % 128, 1) if c != q else packed
-            inverse = jnp.where(in_lanes, moved, 0.0)
-            d = d_ref[c]
-            scaled = jnp.dot(inverse, d, precision=HIGH, preferred_element_type=jnp.float32)
+            inverse = turned[(0 - c) % 4]
+            for t in range(1, 4):
+                inverse = jnp.where(segment == t, turned[(t - c) % 4], inverse)
+            a, b, e = split3(inverse)
+            none = jnp.zeros_like(a)
+            lhs = jnp.concatenate(
+                [
+                    jnp.where(segment == 2, b, a),
+                    jnp.where(segment == 0, e, jnp.where(segment == 1, b, none)),
+                ],
+                axis=1,
+            )
+            rows = d_ref[c, lo:hi, :]
+            rhs = jnp.concatenate([rhs_terms(rows), pad], axis=0)
+            scaled = jnp.dot(lhs, rhs, preferred_element_type=jnp.float32)
             scaled = jnp.where(in_lanes, inverse, scaled)
-            parts = ([jnp.zeros((lo, 128), jnp.float32)] if lo else []) + [scaled]
-            parts += [jnp.zeros((128 - hi, 128), jnp.float32)] if hi < 128 else []
-            full = jnp.concatenate(parts, axis=0) if len(parts) > 1 else scaled
-            lhs = jnp.where(in_cols & ~in_rows, -d, 0.0)
-            kept = jnp.where(in_cols | in_rows, 0.0, d) + full
-            d_ref[c] = kept + jnp.dot(lhs, full, precision=HIGH, preferred_element_type=jnp.float32)
-
-
-def split3(x):
-    a = x.astype(jnp.bfloat16)
-    x = x - a.astype(jnp.float32)
-    b = x.astype(jnp.bfloat16)
-    return a, b, (x - b.astype(jnp.float32)).astype(jnp.bfloat16)
-
-
-def lhs_terms(x):
-    a, b, c = split3(x)
-    return jnp.concatenate([a, a, b, a, c, b], axis=1)
-
-
-def rhs_terms(x):
-    a, b, c = split3(x)
-    return jnp.concatenate([a, b, a, c, a, b], axis=0)
+            a, b, e = split3(jnp.where(in_lanes, 0.0, jnp.where(lane32 < lo, rows, -rows)))
+            lhs = jnp.concatenate([a, a, b, a, e, b, pad], axis=0)
+            rhs = jnp.concatenate([rhs_terms(scaled), pad], axis=0)
+            change = lax.dot_general(
+                lhs, rhs, (((0,), (0,)), ((), ())), preferred_element_type=jnp.float32
+            )
+            d_ref[c] = jnp.where(in_cols, 0.0, d_ref[c]) + change
+            d_ref[c, lo:hi, :] = scaled
 
 
 LOWER = ((0, 0), (1, 0), (1, 1), (2, 0), (2, 1), (2, 2))
@@ -345,8 +369,10 @@
     peer = jnp.arange(yz_count, dtype=jnp.int32)[None, :, None]
     first = jnp.min(jnp.where(mine, peer, yz_count - 1), axis=(1, 2))
     second = jnp.max(jnp.where(mine, peer, 0), axis=(1, 2))
-    placed = place_blocks(fine_blocks, target, widths, yz_count)
-    interp, update = solve(exchange_gram(placed, jnp.stack([first, second]), pivots))
+    goes = target[None, :] == jnp.arange(yz_count, dtype=jnp.int32)[:, None]
+    numbers = jnp.stack([jnp.arange(blocks_dev, dtype=jnp.int32), widths])
+    slots = jnp.sum(jnp.where(goes[None], numbers[:, None, :], 0), axis=2)
+    interp, update = solve(exchange_gram(fine_blocks, slots, jnp.stack([first, second]), pivots))
     return interp, gather_schur(update, from_sides(update), neighbours)
 
 

time: 415 us -> 386 us (0.930)
  Pallas kernels: 358 us -> 337 us
  waiting for transfers between devices: 34.8 us -> 27.9 us
    ppermute x2, waiting for transfers between devices: 29 us -> 1.29 us  [from_sides(): lax.ppermute(x, axis, up)]
    ppermute x2, waiting for transfers between devices: 5.77 us -> 26.6 us  [from_sides(): lax.ppermute(x, axis, [(b, a) for a, b in up])]
    pallas_call x1 -> x0, Pallas kernels: 12.1 us -> none  [place_blocks(): pl.pallas_call(place_kernel, out_shape=jax.ShapeDtypeStruct((peers, rows,...]
    pallas_call x1, Pallas kernels: 51.2 us -> 43 us  [solve(): pl.pallas_call(solve_kernel, out_shape=(jax.ShapeDtypeStruct((clusters, k...]
  transfers between devices with their start and end apart: 4 -> 4, of which waited for: 4 -> 2; matrix products, arithmetic and copies ran while one was open for 0% -> 0% of each run, Pallas kernels for 0% -> 0%
where the time goes in v4:
time: 386 us; the launch traced here: 382 us
  Pallas kernels  337 us (87%)
  waiting for transfers between devices  27.9 us (7%)
  starting transfers between devices  10.3 us (3%)
  local copies, waits for them, and re-layouts  4.15 us (1%)
    pallas_call x1, Pallas kernels, exchange_gram(): pl.pallas_call(exchange_gram_kernel, out_shape=jax.ShapeDtypeStruct((clus...  289 us
    pallas_call x1, Pallas kernels, solve(): pl.pallas_call(solve_kernel, out_shape=(jax.ShapeDtypeStruct((clusters, k...  43 us
    ppermute x2, waiting for transfers between devices, from_sides(): lax.ppermute(x, axis, [(b, a) for a, b in up])  26.6 us
  transfers between devices with their start and end apart: 4, of which 2 were waited for; matrix products, arithmetic and copies ran while one was open for 0% of the time, Pallas kernels for 0%

profile of v4, /device:TPU:10, one launch (start us, length us, event | category | flops | bytes accessed | tf_op | source)
XLA Modules:
  0.0 382.4 jit_solution(18319887741382655640)
XLA Ops:
  0.6 0.8 reshape.33
  1.4 0.1 copy.18
  1.5 1.3 broadcast_in_dim.58.piv_ref
  2.9 0.2 dynamic-slice_reduce_fusion
  3.1 0.1 iota_compare_fusion.1
  3.1 0.7 pad_add_fusion.1
  3.8 0.2 select_reduce_fusion.1
  4.1 0.6 pad_add_fusion.sel_ref
  4.6 0.6 select_reduce_fusion.2.slot_ref
  5.2 288.5 %exchange_gram.1.g_ref = f32[4,384,1024]{2,1,0:T(8,128)} custom-call(s32[2,4]{1,0:T(2,128)} %pad_add_fusion.sel_ref, s32[2,16]{1,0:T(2,128)} %select_reduce_fusion.2.slot_ref, bf16[8,1536,512]{2,1,0:T(8,128)(2,1)} %x_ref.1, s32[4,1,1024]{2,1,0:T(1,128)} %broadcast_in_dim.58.piv_ref), custom_call_target="tpu_custom_call" | custom-call | tf_op jit(solution)/shard_map/exchange_gram/pallas_call | solution.py:136
  293.8 0.0 copy-start.2
  293.8 43.0 %solve_update.1 = (f32[4,384,640]{2,1,0:T(8,128)}, f32[4,6,128,128]{3,2,1,0:T(8,128)}) custom-call(f32[4,384,1024]{2,1,0:T(8,128)} %exchange_gram.1.g_ref), custom_call_target="tpu_custom_call" | custom-call | tf_op jit(solution)/shard_map/solve_update/pallas_call | solution.py:304
  336.8 1.9 collective-permute-start.3
  338.7 4.1 %collective-permute-start.2 = (f32[4,6,128,128]{3,2,1,0:T(8,128)}, f32[4,6,128,128]{3,2,1,0:T(8,128)S(1)}, u32[]{:S(2)}, u32[]{:S(2)}) collective-permute-start(f32[4,6,128,128]{3,2,1,0:T(8,128)} %get-tuple-element.5.own_ref), channel_id=1, source_target_pairs={{0,1},{1,2},{2,3},{3,4},{4,5},{5,6},{6,7},{7,8},{8,9},{9,10},{10,1... | collective-permute-start | bytes 4718600 | tf_op jit(solution)/shard_map/ppermute | solution.py:354
  342.8 1.9 collective-permute-start.1
  344.7 2.4 collective-permute-start
  347.2 0.0 copy-done.2
  347.2 0.6 reshape.34.n_ref
  347.8 26.6 %collective-permute-done.3.d_ref = f32[4,6,128,128]{3,2,1,0:T(8,128)S(1)} collective-permute-done((f32[4,6,128,128]{3,2,1,0:T(8,128)}, f32[4,6,128,128]{3,2,1,0:T(8,128)S(1)}, u32[]{:S(2)}, u32[]{:S(2)}) %collective-permute-start.3) | collective-permute-done | bytes 1572896 | tf_op jit(solution)/shard_map/ppermute | solution.py:354
  374.4 0.0 copy-start
  374.4 1.3 collective-permute-done.2.c_ref
  375.7 0.0 copy-start.1
  375.7 0.0 collective-permute-done.1.b_ref
  375.7 0.0 collective-permute-done.a_ref
  375.7 0.0 copy-done
  375.7 1.1 copy-done.1
  376.8 5.6 %gather_schur.1 = f32[4,384,384]{2,1,0:T(8,128)} custom-call(s32[16]{0:T(128)} %reshape.34.n_ref, f32[4,6,128,128]{3,2,1,0:T(8,128)} %get-tuple-element.5.own_ref, f32[4,6,128,128]{3,2,1,0:T(8,128)} %collective-permute-done.a_ref, f32[4,6,128,128]{3,2,1,0:T(8,128)} %collective-permute-done.1.b_ref, f32[4,6,128,128]{3,2,1,0:T(8,128)} %copy-done.1, ...), custom_call_target="tpu_custom_call" | custom-call | tf_op jit(solution)/shard_map/gather_schur/pallas_call | solution.py:336
  (5 shorter events, 0.0 us)
Async XLA Ops:
  293.8 53.4 %copy-start.2 = (s32[4,4]{1,0:T(4,128)S(1)}, s32[4,4]{1,0:T(4,128)}, u32[]{:S(2)}) copy-start(s32[4,4]{1,0:T(4,128)} %param.9) | copy-start | bytes 196
  336.8 37.6 %collective-permute-start.3 = (f32[4,6,128,128]{3,2,1,0:T(8,128)}, f32[4,6,128,128]{3,2,1,0:T(8,128)S(1)}, u32[]{:S(2)}, u32[]{:S(2)}) collective-permute-start(f32[4,6,128,128]{3,2,1,0:T(8,128)} %get-tuple-element.5.own_ref), channel_id=1, source_target_pairs={{1,0},{2,1},{3,2},{4,3},{5,4},{6,5},{7,6},{8,7},{9,8},{10,9},{11,1... | collective-permute-start | bytes 4718600 | tf_op jit(solution)/shard_map/ppermute | solution.py:354
  338.7 37.0 %collective-permute-start.2 = (f32[4,6,128,128]{3,2,1,0:T(8,128)}, f32[4,6,128,128]{3,2,1,0:T(8,128)S(1)}, u32[]{:S(2)}, u32[]{:S(2)}) collective-permute-start(f32[4,6,128,128]{3,2,1,0:T(8,128)} %get-tuple-element.5.own_ref), channel_id=1, source_target_pairs={{0,1},{1,2},{2,3},{3,4},{4,5},{5,6},{6,7},{7,8},{8,9},{9,10},{10,1... | collective-permute-start | bytes 4718600 | tf_op jit(solution)/shard_map/ppermute | solution.py:354
  342.8 32.9 %collective-permute-start.1 = (f32[4,6,128,128]{3,2,1,0:T(8,128)}, f32[4,6,128,128]{3,2,1,0:T(8,128)}, u32[]{:S(2)}, u32[]{:S(2)}) collective-permute-start(f32[4,6,128,128]{3,2,1,0:T(8,128)} %get-tuple-element.5.own_ref), channel_id=1, source_target_pairs={{16,0},{32,16},{48,32},{64,48},{80,64},{96,80},{112,96},{17,1},{33... | collective-permute-start | bytes 4718600 | tf_op jit(solution)/shard_map/ppermute | solution.py:354
  344.7 30.9 %collective-permute-start = (f32[4,6,128,128]{3,2,1,0:T(8,128)}, f32[4,6,128,128]{3,2,1,0:T(8,128)}, u32[]{:S(2)}, u32[]{:S(2)}) collective-permute-start(f32[4,6,128,128]{3,2,1,0:T(8,128)} %get-tuple-element.5.own_ref), channel_id=1, source_target_pairs={{0,16},{16,32},{32,48},{48,64},{64,80},{80,96},{96,112},{1,17},{17... | collective-permute-start | bytes 4718600 | tf_op jit(solution)/shard_map/ppermute | solution.py:354
  374.4 1.3 copy-start
  375.7 1.1 copy-start.1

commit v5 on v4

--- a/solution.py
+++ b/solution.py
@@ -95,7 +95,7 @@
     launch(1)
 
     def make_hot(c, carry):
-        hot_ref[c] = jnp.where(iota((width, width), 0) == piv_ref[c], 1.0, 0.0).astype(hot_ref.dtype)
+        hot_ref[c] = jnp.where(iota((width, width), 0) == piv_ref[pl.ds(c, 1), :], 1.0, 0.0).astype(hot_ref.dtype)
         return carry
 
     lax.fori_loop(0, clusters, make_hot, 0)
@@ -150,7 +150,7 @@
             collective_id=0, has_side_effects=True, vmem_limit_bytes=63 * 1024 * 1024
         ),
         name="exchange_gram",
-    )(chosen, slots, fine_blocks, pivots[:, None, :])
+    )(chosen, slots, fine_blocks, pivots)
 
 
 def packed_inverse(s):
@@ -251,108 +251,151 @@
             d_ref[c, lo:hi, :] = scaled
 
 
-LOWER = ((0, 0), (1, 0), (1, 1), (2, 0), (2, 1), (2, 2))
-
-
-def solve_kernel(g_ref, interp_ref, update_ref, w_ref, d_ref):
+def solve_kernel(g_ref, interp_ref, w_ref, d_ref):
     clusters, width = g_ref.shape[0], g_ref.shape[2]
     w_ref[...] = g_ref[...]
-
-    def eliminate(s, carry):
-        at = pl.ds(pl.multiple_of(s * 128, 128), 128)
+    for s in range(K // 128):
+        lo, hi = 128 * s, 128 * s + 128
         for c in range(clusters):
-            d_ref[c] = w_ref[c, at, at]
+            d_ref[c] = w_ref[c, lo:hi, lo:hi]
         invert_diagonal(d_ref)
 
         def one(c, carry):
             scaled = jnp.dot(
-                lhs_terms(d_ref[c]), rhs_terms(w_ref[c, at, :]), preferred_element_type=jnp.float32
+                lhs_terms(d_ref[c]), rhs_terms(w_ref[c, lo:hi, hi:]), preferred_element_type=jnp.float32
             )
-            w_ref[c, at, :] = scaled
             terms = rhs_terms(scaled)
-            for far in range(1, K // 128):
-                other = lax.rem(s + far, K // 128)
-                rows = pl.ds(pl.multiple_of(other * 128, 128), 128)
-                w_ref[c, rows, :] = w_ref[c, rows, :] - jnp.dot(
-                    lhs_terms(w_ref[c, rows, at]), terms, preferred_element_type=jnp.float32
-                )
+            out = interp_ref if hi == K else w_ref
+            out[c, lo:hi, 0 if hi == K else hi :] = scaled
+            for t in range(K // 128):
+                if t != s:
+                    rows = slice(128 * t, 128 * t + 128)
+                    rest = w_ref[c, rows, hi:] - jnp.dot(
+                        lhs_terms(w_ref[c, rows, lo:hi]), terms, preferred_element_type=jnp.float32
+                    )
+                    out[c, rows, 0 if hi == K else hi :] = rest
             return carry
 
-        return lax.fori_loop(0, clusters, one, carry)
-
-    lax.fori_loop(0, K // 128, eliminate, 0)
-
-    def finish(c, carry):
-        x = w_ref[c, :, K:]
-        interp_ref[c] = x
-        a, b, _ = split3(x)
+        lax.fori_loop(0, clusters, one, 0)
+
+
+def solve(gram):
+    clusters, kept, width = gram.shape
+    vmem = pl.BlockSpec(memory_space=pltpu.VMEM)
+    return pl.pallas_call(
+        solve_kernel,
+        out_shape=jax.ShapeDtypeStruct((clusters, kept, width - kept), jnp.float32),
+        in_specs=[vmem],
+        out_specs=vmem,
+        scratch_shapes=[
+            pltpu.VMEM((clusters, kept, width), jnp.float32),
+            pltpu.VMEM((clusters, 128, 128), jnp.float32),
+        ],
+        compiler_params=pltpu.CompilerParams(vmem_limit_bytes=56 * 1024 * 1024),
+        name="solve",
+    )(gram)
+
+
+PACKED = 648
+
+
+def mirrored(low):
+    at = iota(low.shape, 0) >= iota(low.shape, 1)
+    return jnp.where(at, low, low.T)
+
+
+def schur_kernel(n_ref, interp_ref, o_ref, own_ref, send_sem, recv_sems, *sides):
+    clusters = own_ref.shape[0]
+    places = []
+    for axis in ("gx", "yz"):
+        here, size = lax.axis_index(axis), lax.axis_size(axis)
+        places += [(axis, here - 1, here > 0), (axis, here + 1, here < size - 1)]
+    barrier = pltpu.get_barrier_semaphore()
+    for axis, to, there in places:
+
+        @pl.when(there)
+        def _():
+            pl.semaphore_signal(
+                barrier, inc=1, device_id={axis: to}, device_id_type=pl.DeviceIdType.MESH
+            )
+
+    count = sum(there.astype(jnp.int32) for _, _, there in places)
+    row, col = iota((128, 128), 0), iota((128, 128), 1)
+
+    def make(c):
+        a, b, _ = split3(interp_ref[c])
         lhs = jnp.concatenate([a, a, b], axis=1)
         rhs = jnp.concatenate([a, b, a], axis=1)
         across = (((1,), (1,)), ((), ()))
         left = lax.dot_general(lhs, rhs[:256], across, preferred_element_type=jnp.float32)
         last = lax.dot_general(lhs[256:], rhs[256:], across, preferred_element_type=jnp.float32)
-        for n, (i, j) in enumerate(LOWER):
-            update_ref[c, n] = last if j == 2 else left[128 * i : 128 * i + 128, 128 * j : 128 * j + 128]
+        own_ref[c, :256] = left[128:, :128]
+        own_ref[c, 256:384] = left[256:, 128:]
+        middle = left[128:256, 128:]
+        own_ref[c, 384:512] = jnp.where(row >= col, left[:128, :128], middle)
+        own_ref[c, 512:640] = last
+        diagonal = jnp.sum(jnp.where(row == col, middle, 0.0), axis=0, keepdims=True)
+        own_ref[c, 640:648] = jnp.broadcast_to(diagonal, (8, 128))
+
+    def copy(c, n):
+        axis, to, _ = places[n]
+        return pltpu.make_async_remote_copy(
+            src_ref=own_ref.at[c],
+            dst_ref=sides[n ^ 1].at[c],
+            send_sem=send_sem.at[n],
+            recv_sem=recv_sems.at[n ^ 1],
+            device_id={axis: to},
+            device_id_type=pl.DeviceIdType.MESH,
+        )
+
+    make(0)
+    pl.semaphore_wait(barrier, count)
+    for c in range(clusters):
+        for n in (2, 3, 0, 1):
+            pl.when(places[n][2])(lambda: copy(c, n).start())
+        if c + 1 < clusters:
+            make(c + 1)
+
+    def settle(sem):
+        pltpu.make_async_copy(own_ref, own_ref, sem).wait()
+
+    for n in range(4):
+        pl.when(places[n][2])(lambda: settle(recv_sems.at[n]))
+
+    def add(c, carry):
+        total = own_ref[c]
+        for n in range(4):
+            total = total + jnp.where(places[n][2], sides[n][n_ref[c, n]], 0.0)
+        for at, i, j in ((0, 1, 0), (128, 2, 0), (256, 2, 1)):
+            x = total[at : at + 128]
+            o_ref[c, 128 * i : 128 * i + 128, 128 * j : 128 * j + 128] = x
+            o_ref[c, 128 * j : 128 * j + 128, 128 * i : 128 * i + 128] = x.T
+        both, last = total[384:512], total[512:640]
+        o_ref[c, :128, :128] = mirrored(both)
+        o_ref[c, 128:256, 128:256] = jnp.where(row == col, total[640:641], mirrored(both.T))
+        o_ref[c, 256:, 256:] = mirrored(last)
         return carry
 
-    lax.fori_loop(0, clusters, finish, 0)
-
-
-def solve(gram):
-    clusters, kept, width = gram.shape
+    lax.fori_loop(0, clusters, add, 0)
+    for n in range(4):
+        pl.when(places[n][2])(lambda: settle(send_sem.at[n]))
+
+
+def schur_of(interp, neighbours):
+    clusters = interp.shape[0]
     vmem = pl.BlockSpec(memory_space=pltpu.VMEM)
-    return pl.pallas_call(
-        solve_kernel,
-        out_shape=(
-            jax.ShapeDtypeStruct((clusters, kept, width - kept), jnp.float32),
-            jax.ShapeDtypeStruct((clusters, len(LOWER), 128, 128), jnp.float32),
-        ),
-        in_specs=[vmem],
-        out_specs=(vmem, vmem),
-        scratch_shapes=[
-            pltpu.VMEM((clusters, kept, width), jnp.float32),
-            pltpu.VMEM((clusters, 128, 128), jnp.float32),
-        ],
-        compiler_params=pltpu.CompilerParams(vmem_limit_bytes=56 * 1024 * 1024),
-        name="solve_update",
-    )(gram)
-
-
-def schur_kernel(n_ref, own_ref, a_ref, b_ref, c_ref, d_ref, o_ref):
-    for n, (i, j) in enumerate(LOWER):
-        x = own_ref[0, n] + ((a_ref[0, n] + b_ref[0, n]) + (c_ref[0, n] + d_ref[0, n]))
-        o_ref[0, 128 * i : 128 * i + 128, 128 * j : 128 * j + 128] = x
-        if i != j:
-            o_ref[0, 128 * j : 128 * j + 128, 128 * i : 128 * i + 128] = x.T
-
-
-def gather_schur(update, sides, neighbours):
-    clusters = update.shape[0]
-    block = (1,) + update.shape[1:]
-
-    def pick(side):
-        return pl.BlockSpec(block, lambda c, n: (n[4 * c + side], 0, 0, 0))
-
+    packed = pltpu.VMEM((clusters, PACKED, 128), jnp.float32)
     return pl.pallas_call(
         schur_kernel,
         out_shape=jax.ShapeDtypeStruct((clusters, K, K), jnp.float32),
-        grid_spec=pltpu.PrefetchScalarGridSpec(
-            num_scalar_prefetch=1,
-            grid=(clusters,),
-            in_specs=[pl.BlockSpec(block, lambda c, n: (c, 0, 0, 0))] + [pick(side) for side in range(4)],
-            out_specs=pl.BlockSpec((1, K, K), lambda c, n: (c, 0, 0)),
+        in_specs=[pl.BlockSpec(memory_space=pltpu.SMEM), vmem],
+        out_specs=vmem,
+        scratch_shapes=[packed, pltpu.SemaphoreType.DMA((4,)), pltpu.SemaphoreType.DMA((4,))] + [packed] * 4,
+        compiler_params=pltpu.CompilerParams(
+            collective_id=1, has_side_effects=True, vmem_limit_bytes=40 * 1024 * 1024
         ),
-        name="gather_schur",
-    )(neighbours.reshape(-1), update, *sides)
-
-
-def from_sides(x):
-    sides = []
-    for axis in ("gx", "yz"):
-        size = lax.axis_size(axis)
-        up = [(i, i + 1) for i in range(size - 1)]
-        sides += [lax.ppermute(x, axis, up), lax.ppermute(x, axis, [(b, a) for a, b in up])]
-    return sides
+        name="update_schur",
+    )(neighbours, interp)
 
 
 def body(fine_blocks, fine_to_coarse, widths, pivots, neighbours):
@@ -372,8 +415,8 @@
     goes = target[None, :] == jnp.arange(yz_count, dtype=jnp.int32)[:, None]
     numbers = jnp.stack([jnp.arange(blocks_dev, dtype=jnp.int32), widths])
     slots = jnp.sum(jnp.where(goes[None], numbers[:, None, :], 0), axis=2)
-    interp, update = solve(exchange_gram(fine_blocks, slots, jnp.stack([first, second]), pivots))
-    return interp, gather_schur(update, from_sides(update), neighbours)
+    interp = solve(exchange_gram(fine_blocks, slots, jnp.stack([first, second]), pivots))
+    return interp, schur_of(interp, neighbours)
 
 
 def solution(mesh):

time: 386 us -> 367 us (0.951)
  waiting for transfers between devices: 27.9 us -> 0 us
  Pallas kernels: 337 us -> 360 us
  starting transfers between devices: 10.3 us -> 0 us
    ppermute x4 -> x0, waiting for transfers between devices: 27.9 us -> none  [the longest x2 26.6 us: from_sides(): lax.ppermute(x, axis, [(b, a) for a, b in up])]
    pallas_call x2, Pallas kernels: 48.6 us -> 71 us  [the longest x1 36.3 us: solve(): pl.pallas_call(solve_kernel, out_shape=jax.ShapeDtypeStruct((clusters, ke...]
    ppermute x4 -> x0, starting transfers between devices: 10.3 us -> none  [the longest x2 6.48 us: from_sides(): lax.ppermute(x, axis, up)]
  transfers between devices with their start and end apart: 4 -> 0, of which waited for: 2 -> 0; matrix products, arithmetic and copies ran while one was open for 0% -> 0% of each run, Pallas kernels for 0% -> 0%
where the time goes in v5:
time: 367 us
  Pallas kernels  360 us (98%)
  local copies, waits for them, and re-layouts  4.56 us (1%)
    pallas_call x1, Pallas kernels, exchange_gram(): pl.pallas_call(exchange_gram_kernel, out_shape=jax.ShapeDtypeStruct((clus...  289 us
    pallas_call x1, Pallas kernels, solve(): pl.pallas_call(solve_kernel, out_shape=jax.ShapeDtypeStruct((clusters, ke...  36.3 us
    pallas_call x1, Pallas kernels, schur_of(): pl.pallas_call(schur_kernel, out_shape=jax.ShapeDtypeStruct((clusters, K,...  34.7 us

profile of v5, /device:TPU:10, one launch (start us, length us, event | category | flops | bytes accessed | tf_op | source)
XLA Modules:
  0.0 367.0 jit_solution(1631384579376588972)
XLA Ops:
  0.6 0.7 pad_add_fusion.1
  1.3 0.8 reshape.30
  2.1 0.1 copy.18
  2.2 0.2 dynamic-slice_reduce_fusion
  2.4 0.2 select_reduce_fusion.1
  2.6 0.6 pad_add_fusion.sel_ref
  3.2 0.1 iota_compare_fusion.1
  3.3 0.6 select_reduce_fusion.2.slot_ref
  3.9 288.5 %exchange_gram.1.g_ref = f32[4,384,1024]{2,1,0:T(8,128)} custom-call(s32[2,4]{1,0:T(2,128)} %pad_add_fusion.sel_ref, s32[2,16]{1,0:T(2,128)} %select_reduce_fusion.2.slot_ref, bf16[8,1536,512]{2,1,0:T(8,128)(2,1)} %x_ref.1, s32[4,1024]{1,0:T(4,128)} %piv_ref.1), custom_call_target="tpu_custom_call" | custom-call | tf_op jit(solution)/shard_map/exchange_gram/pallas_call | solution.py:136
  292.5 0.0 copy-start.1
  292.5 36.3 %solve.1.interp_ref = f32[4,384,640]{2,1,0:T(8,128)} custom-call(f32[4,384,1024]{2,1,0:T(8,128)} %exchange_gram.1.g_ref), custom_call_target="tpu_custom_call" | custom-call | tf_op jit(solution)/shard_map/solve/pallas_call | solution.py:285
  328.8 0.0 copy-done.1
  328.8 0.0 copy-start
  328.8 2.1 copy-done
  330.9 34.7 %update_schur.1 = f32[4,384,384]{2,1,0:T(8,128)S(1)} custom-call(s32[4,4]{1,0:T(4,128)S(1)} %copy-done.1, f32[4,384,640]{2,1,0:T(8,128)S(1)} %copy-done), custom_call_target="tpu_custom_call" | custom-call | tf_op jit(solution)/shard_map/update_schur/pallas_call | solution.py:388
  365.6 1.4 copy.20
  (5 shorter events, 0.0 us)
Async XLA Ops:
  292.5 36.3 %copy-start.1 = (s32[4,4]{1,0:T(4,128)S(1)}, s32[4,4]{1,0:T(4,128)}, u32[]{:S(2)}) copy-start(s32[4,4]{1,0:T(4,128)} %n_ref.1) | copy-start | bytes 196
  328.8 2.1 copy-start

commit v6 on v5

--- a/solution.py
+++ b/solution.py
@@ -15,26 +15,34 @@
     return lax.broadcasted_iota(jnp.int32, shape, dim)
 
 
-GROUPS, PIECES, STAGES = 6, 4, 3
+SHARES = (1, 2, 2, 2, 2, 2, 1)
+STARTS = tuple(sum(SHARES[:n]) for n in range(len(SHARES)))
+GROUPS, STAGES = len(SHARES), 3
 
 
 def exchange_gram_kernel(
-    sel_ref, slot_ref, x_ref, piv_ref, o_ref, hot_ref, send_sems, recv_sems, in_sems, *bufs
+    sel_ref, slot_ref, x_ref, piv_ref, g_ref, o_ref, hot_ref, send_sems, recv_sems, in_sems, out_sems, *bufs
 ):
     lands, slots, blocks = bufs[:GROUPS], bufs[GROUPS : GROUPS + STAGES], bufs[GROUPS + STAGES :]
     me = lax.axis_index("yz")
     plane = lax.axis_size("yz")
     side = 4
     clusters, kept, width = o_ref.shape
-    peers, height, half = lands[0].shape
-    step = height // PIECES
+    peers, unit, half = lands[0].shape
+    step = unit // 2
 
     def peer(d):
         return lax.rem(me // side + d // side, plane // side) * side + lax.rem(me + d, side)
 
+    def done(c):
+        return pltpu.make_async_copy(o_ref.at[c], g_ref.at[c], out_sems.at[c])
+
     def fetch(group):
+        height = SHARES[group] * unit
         return pltpu.make_async_copy(
-            x_ref.at[:, pl.ds(group * height, height)], blocks[group % 2], in_sems.at[group % 2]
+            x_ref.at[:, pl.ds(STARTS[group] * unit, height)],
+            blocks[group % 2].at[:, pl.ds(0, height)],
+            in_sems.at[group % 2],
         )
 
     fetch(0).start()
@@ -50,21 +58,22 @@
     lax.fori_loop(1, peers, greet, 0)
 
     def sent(group):
-        rest = slots[group % STAGES].at[pl.ds(0, peers - 1)]
+        rest = slots[group % STAGES].at[pl.ds(0, peers - 1), pl.ds(0, SHARES[group] * unit)]
         pltpu.make_async_copy(rest, rest, send_sems.at[group % STAGES]).wait()
 
     def fill(group):
         fetch(group).wait()
         if group >= STAGES:
             sent(group - STAGES)
+        height = SHARES[group] * unit
         column = iota((height, half), 1)
 
         def masked(t):
-            x = blocks[group % 2][slot_ref[0, t]]
+            x = blocks[group % 2][slot_ref[0, t], :height]
             return jnp.where(column < slot_ref[1, t], x, jnp.zeros_like(x))
 
         def one(d, carry):
-            slots[group % STAGES][peer(d)] = masked(peer(d))
+            slots[group % STAGES][peer(d), :height] = masked(peer(d))
             return carry
 
         lax.fori_loop(1, peers, one, 0)
@@ -86,7 +95,7 @@
             ).start()
             return carry
 
-        lax.fori_loop(0, PIECES * (peers - 1), one, 0)
+        lax.fori_loop(0, SHARES[group] * unit // step * (peers - 1), one, 0)
 
     fill(0)
     pl.semaphore_wait(barrier, peers - 1)
@@ -117,6 +126,8 @@
                 pivoted[:, :kept], pivoted, (((0,), (0,)), ((), ())), preferred_element_type=jnp.float32
             )
             o_ref[c] = part if group == 0 else o_ref[c] + part
+            if group == GROUPS - 1:
+                done(c).start()
             return carry
 
         lax.fori_loop(0, clusters, one_cluster, 0)
@@ -125,27 +136,32 @@
 
     for group in range(GROUPS - STAGES, GROUPS):
         sent(group)
+    for c in range(clusters):
+        done(c).wait()
 
 
 def exchange_gram(fine_blocks, slots, chosen, pivots):
     count, rows, half = fine_blocks.shape
     peers = slots.shape[1]
     clusters, width = pivots.shape
-    height = rows // GROUPS
+    unit = rows // sum(SHARES)
     vmem, smem = pl.BlockSpec(memory_space=pltpu.VMEM), pl.BlockSpec(memory_space=pltpu.SMEM)
     return pl.pallas_call(
         exchange_gram_kernel,
         out_shape=jax.ShapeDtypeStruct((clusters, K, width), jnp.float32),
         in_specs=[smem, smem, pl.BlockSpec(memory_space=pltpu.HBM), vmem],
-        out_specs=vmem,
+        out_specs=pl.BlockSpec(memory_space=pltpu.HBM),
         scratch_shapes=[
+            pltpu.VMEM((clusters, K, width), jnp.float32),
             pltpu.VMEM((clusters, width, width), jnp.bfloat16),
             pltpu.SemaphoreType.DMA((STAGES,)),
             pltpu.SemaphoreType.DMA((GROUPS,)),
             pltpu.SemaphoreType.DMA((2,)),
+            pltpu.SemaphoreType.DMA((clusters,)),
         ]
-        + [pltpu.VMEM((peers, height, half), jnp.bfloat16) for _ in range(GROUPS + STAGES)]
-        + [pltpu.VMEM((count, height, half), jnp.bfloat16) for _ in range(2)],
+        + [pltpu.VMEM((peers, share * unit, half), jnp.bfloat16) for share in SHARES]
+        + [pltpu.VMEM((peers, max(SHARES) * unit, half), jnp.bfloat16) for _ in range(STAGES)]
+        + [pltpu.VMEM((count, max(SHARES) * unit, half), jnp.bfloat16) for _ in range(2)],
         compiler_params=pltpu.CompilerParams(
             collective_id=0, has_side_effects=True, vmem_limit_bytes=63 * 1024 * 1024
         ),
@@ -251,14 +267,21 @@
             d_ref[c, lo:hi, :] = scaled
 
 
-def solve_kernel(g_ref, interp_ref, w_ref, d_ref):
-    clusters, width = g_ref.shape[0], g_ref.shape[2]
-    w_ref[...] = g_ref[...]
+def solve_kernel(g_ref, interp_ref, w_ref, d_ref, sems):
+    clusters = g_ref.shape[0]
+    first = pltpu.make_async_copy(g_ref.at[:, pl.ds(0, 128), pl.ds(0, 128)], d_ref, sems.at[0])
+    rest = pltpu.make_async_copy(g_ref, w_ref, sems.at[1])
+    first.start()
+    rest.start()
+    first.wait()
     for s in range(K // 128):
         lo, hi = 128 * s, 128 * s + 128
-        for c in range(clusters):
-            d_ref[c] = w_ref[c, lo:hi, lo:hi]
+        if s > 0:
+            for c in range(clusters):
+                d_ref[c] = w_ref[c, lo:hi, lo:hi]
         invert_diagonal(d_ref)
+        if s == 0:
+            rest.wait()
 
         def one(c, carry):
             scaled = jnp.dot(
@@ -285,11 +308,12 @@
     return pl.pallas_call(
         solve_kernel,
         out_shape=jax.ShapeDtypeStruct((clusters, kept, width - kept), jnp.float32),
-        in_specs=[vmem],
+        in_specs=[pl.BlockSpec(memory_space=pltpu.HBM)],
         out_specs=vmem,
         scratch_shapes=[
             pltpu.VMEM((clusters, kept, width), jnp.float32),
             pltpu.VMEM((clusters, 128, 128), jnp.float32),
+            pltpu.SemaphoreType.DMA((2,)),
         ],
         compiler_params=pltpu.CompilerParams(vmem_limit_bytes=56 * 1024 * 1024),
         name="solve",
@@ -304,8 +328,14 @@
     return jnp.where(at, low, low.T)
 
 
-def schur_kernel(n_ref, interp_ref, o_ref, own_ref, send_sem, recv_sems, *sides):
+def schur_kernel(n_ref, interp_ref, o_ref, x_ref, own_ref, in_sems, send_sem, recv_sems, *sides):
     clusters = own_ref.shape[0]
+
+    def fetch(c):
+        return pltpu.make_async_copy(interp_ref.at[c], x_ref.at[c], in_sems.at[c])
+
+    for c in range(clusters):
+        fetch(c).start()
     places = []
     for axis in ("gx", "yz"):
         here, size = lax.axis_index(axis), lax.axis_size(axis)
@@ -323,7 +353,8 @@
     row, col = iota((128, 128), 0), iota((128, 128), 1)
 
     def make(c):
-        a, b, _ = split3(interp_ref[c])
+        fetch(c).wait()
+        a, b, _ = split3(x_ref[c])
         lhs = jnp.concatenate([a, a, b], axis=1)
         rhs = jnp.concatenate([a, b, a], axis=1)
         across = (((1,), (1,)), ((), ()))
@@ -388,11 +419,18 @@
     return pl.pallas_call(
         schur_kernel,
         out_shape=jax.ShapeDtypeStruct((clusters, K, K), jnp.float32),
-        in_specs=[pl.BlockSpec(memory_space=pltpu.SMEM), vmem],
+        in_specs=[pl.BlockSpec(memory_space=pltpu.SMEM), pl.BlockSpec(memory_space=pltpu.HBM)],
         out_specs=vmem,
-        scratch_shapes=[packed, pltpu.SemaphoreType.DMA((4,)), pltpu.SemaphoreType.DMA((4,))] + [packed] * 4,
+        scratch_shapes=[
+            pltpu.VMEM(interp.shape, jnp.float32),
+            packed,
+            pltpu.SemaphoreType.DMA((clusters,)),
+            pltpu.SemaphoreType.DMA((4,)),
+            pltpu.SemaphoreType.DMA((4,)),
+        ]
+        + [packed] * 4,
         compiler_params=pltpu.CompilerParams(
-            collective_id=1, has_side_effects=True, vmem_limit_bytes=40 * 1024 * 1024
+            collective_id=1, has_side_effects=True, vmem_limit_bytes=62 * 1024 * 1024
         ),
         name="update_schur",
     )(neighbours, interp)

time: 367 us -> 364 us (level)
  no operation moved by 1% of the time
where the time goes in v6:
time: 364 us
  Pallas kernels  357 us (98%)
  local copies, waits for them, and re-layouts  4.26 us (1%)
    pallas_call x1, Pallas kernels, exchange_gram(): pl.pallas_call(exchange_gram_kernel, out_shape=jax.ShapeDtypeStruct((clus...  286 us
    pallas_call x1, Pallas kernels, schur_of(): pl.pallas_call(schur_kernel, out_shape=jax.ShapeDtypeStruct((clusters, K,...  36.3 us
    pallas_call x1, Pallas kernels, solve(): pl.pallas_call(solve_kernel, out_shape=jax.ShapeDtypeStruct((clusters, ke...  34.2 us

profile of v6, /device:TPU:10, one launch (start us, length us, event | category | flops | bytes accessed | tf_op | source)
XLA Modules:
  0.0 363.9 jit_solution(12400427149883659341)
XLA Ops:
  0.6 0.7 pad_add_fusion.1
  1.3 0.8 reshape.30
  2.1 0.1 copy.18
  2.2 0.2 dynamic-slice_reduce_fusion
  2.4 0.2 select_reduce_fusion.1
  2.6 0.6 pad_add_fusion.sel_ref
  3.2 0.1 iota_compare_fusion.1
  3.3 0.6 select_reduce_fusion.2.slot_ref
  3.9 286.2 %exchange_gram.1.g_ref = f32[4,384,1024]{2,1,0:T(8,128)} custom-call(s32[2,4]{1,0:T(2,128)} %pad_add_fusion.sel_ref, s32[2,16]{1,0:T(2,128)} %select_reduce_fusion.2.slot_ref, bf16[8,1536,512]{2,1,0:T(8,128)(2,1)} %x_ref.1, s32[4,1024]{1,0:T(4,128)} %piv_ref.1), custom_call_target="tpu_custom_call" | custom-call | tf_op jit(solution)/shard_map/exchange_gram/pallas_call | solution.py:149
  290.2 34.2 %solve.1.interp_ref = f32[4,384,640]{2,1,0:T(8,128)} custom-call(f32[4,384,1024]{2,1,0:T(8,128)} %exchange_gram.1.g_ref), custom_call_target="tpu_custom_call" | custom-call | tf_op jit(solution)/shard_map/solve/pallas_call | solution.py:308
  324.4 36.3 %update_schur.1 = f32[4,384,384]{2,1,0:T(8,128)} custom-call(s32[4,4]{1,0:T(4,128)} %n_ref.1, f32[4,384,640]{2,1,0:T(8,128)} %solve.1.interp_ref), custom_call_target="tpu_custom_call" | custom-call | tf_op jit(solution)/shard_map/update_schur/pallas_call | solution.py:419
  360.7 3.2 copy.20
  (5 shorter events, 0.0 us)

commit v7 on v6

--- a/solution.py
+++ b/solution.py
@@ -430,7 +430,7 @@
         ]
         + [packed] * 4,
         compiler_params=pltpu.CompilerParams(
-            collective_id=1, has_side_effects=True, vmem_limit_bytes=62 * 1024 * 1024
+            collective_id=1, has_side_effects=True, vmem_limit_bytes=49 * 1024 * 1024
         ),
         name="update_schur",
     )(neighbours, interp)

time: 364 us -> 361 us (level)
  no operation moved by 1% of the time
where the time goes in v7:
time: 361 us
  Pallas kernels  355 us (98%)
    pallas_call x1, Pallas kernels, exchange_gram(): pl.pallas_call(exchange_gram_kernel, out_shape=jax.ShapeDtypeStruct((clus...  286 us
    pallas_call x1, Pallas kernels, schur_of(): pl.pallas_call(schur_kernel, out_shape=jax.ShapeDtypeStruct((clusters, K,...  34.8 us
    pallas_call x1, Pallas kernels, solve(): pl.pallas_call(solve_kernel, out_shape=jax.ShapeDtypeStruct((clusters, ke...  34.2 us

profile of v7, /device:TPU:10, one launch (start us, length us, event | category | flops | bytes accessed | tf_op | source)
XLA Modules:
  0.0 360.6 jit_solution(10715210537587394722)
XLA Ops:
  0.6 0.7 pad_add_fusion.1
  1.3 0.8 reshape.30
  2.1 0.1 copy.18
  2.2 0.2 dynamic-slice_reduce_fusion
  2.4 0.2 select_reduce_fusion.1
  2.6 0.6 pad_add_fusion.sel_ref
  3.2 0.1 iota_compare_fusion.1
  3.3 0.6 select_reduce_fusion.2.slot_ref
  3.9 286.2 %exchange_gram.1.g_ref = f32[4,384,1024]{2,1,0:T(8,128)} custom-call(s32[2,4]{1,0:T(2,128)} %pad_add_fusion.sel_ref, s32[2,16]{1,0:T(2,128)} %select_reduce_fusion.2.slot_ref, bf16[8,1536,512]{2,1,0:T(8,128)(2,1)} %x_ref.1, s32[4,1024]{1,0:T(4,128)} %piv_ref.1), custom_call_target="tpu_custom_call" | custom-call | tf_op jit(solution)/shard_map/exchange_gram/pallas_call | solution.py:149
  290.2 0.0 copy-start
  290.2 34.2 %solve.1.interp_ref = f32[4,384,640]{2,1,0:T(8,128)} custom-call(f32[4,384,1024]{2,1,0:T(8,128)} %exchange_gram.1.g_ref), custom_call_target="tpu_custom_call" | custom-call | tf_op jit(solution)/shard_map/solve/pallas_call | solution.py:308
  324.4 0.0 copy-done
  324.4 34.8 %update_schur.1 = f32[4,384,384]{2,1,0:T(8,128)S(1)} custom-call(s32[4,4]{1,0:T(4,128)S(1)} %copy-done, f32[4,384,640]{2,1,0:T(8,128)} %solve.1.interp_ref), custom_call_target="tpu_custom_call" | custom-call | tf_op jit(solution)/shard_map/update_schur/pallas_call | solution.py:419
  359.2 1.4 copy.20
  (5 shorter events, 0.0 us)
Async XLA Ops:
  290.2 34.2 %copy-start = (s32[4,4]{1,0:T(4,128)S(1)}, s32[4,4]{1,0:T(4,128)}, u32[]{:S(2)}) copy-start(s32[4,4]{1,0:T(4,128)} %n_ref.1) | copy-start | bytes 196
